TPU v7x, 256 devices: a whole 4x4x8 slice. The times are simulated.
256 devices in a mesh: seq: 64 (over z, x, core), head: 4 (over y).
Axes of the slice: x: 4, y: 4, z: 8, core: 2. Of those that a mesh axis runs over, the one named last changes fastest.
Arguments:
- tokens: bfloat16 [65536, 2048], P('seq', 'head'), may hold values from -8 to 8
- w_query: bfloat16 [2048, 2048], P(None, 'head'), may hold values from -1 to 1, as said below
- w_key: bfloat16 [2048, 2048], P(None, 'head'), may hold values from -1 to 1, as said below
- w_value: bfloat16 [2048, 2048], P(None, 'head'), may hold values from -0.125 to 0.125
- w_out: bfloat16 [2048, 2048], P('head'), may hold values from -0.125 to 0.125
- mix_logit: float32 [8], P('head'), may hold values from -2 to 2
Outputs:
- layer_out: bfloat16 [65536, 2048], P('seq', 'head')
Inputs may be any that keep to these rules, and one draw needn't show every extreme that they name: `w_query`: entries of mean zero with a standard deviation of about 2048 ** -0.5. `w_key`: entries of mean zero with a standard deviation of about 2048 ** -0.5.
All inputs are finite; a program needn't handle non-finite values.
Results may differ from a plain program's by a relative error of at most 0.0065.
Values may be sent and summed in bfloat16 or wider, within the bound.
A program may use at most 128 MiB of HBM per device.

v0:
```python
import jax
import jax.numpy as jnp
from jax import lax
from jax.sharding import Mesh
from jax.sharding import PartitionSpec as P

SEQ = ("seq_0", "seq_1", "seq_2")


def nothing_yet(shard, identity):
    return jax.tree.map(
        lambda a, e: jnp.broadcast_to(jnp.asarray(e, a.dtype), a.shape), shard, identity
    )


def carried_in(shard, axes, combine, identity):
    before = start = nothing_yet(shard, identity)
    running = shard
    for axis in reversed(axes):
        length, mine = (lax.axis_size(axis), lax.axis_index(axis))
        pieces = jax.tree.map(
            lambda part, kind: lax.all_gather(part.astype(kind), axis),
            running,
            (jnp.bfloat16, jnp.bfloat16),
        )
        inside, running = (start, start)
        for k in range(length):
            passed = k < mine
            running = combine(
                running, jax.tree.map(lambda part, own: part[k].astype(own.dtype), pieces, shard)
            )
            inside = jax.tree.map(lambda new, old: jnp.where(passed, new, old), running, inside)
        before = combine(inside, before)
    return before


def feature(values):
    return jax.nn.elu(values) + 1.0


def add_pairs(earlier, later):
    return (earlier[0] + later[0], earlier[1] + later[1])


def on_device(tokens, w_query, w_key, w_value, w_out, mix_logit):
    seg = tokens.shape[0]
    heads = mix_logit.shape[0]
    width = w_query.shape[1]
    hsize = width // heads
    empty = jnp.zeros((seg, width), jnp.float32)
    totals = (empty, empty, empty)
    piece = lax.all_gather(tokens, "head", axis=1, tiled=True)
    result = []
    for total, weight in zip(totals, (w_query, w_key, w_value)):
        result.append(jnp.dot(piece, weight, preferred_element_type=jnp.float32))
    query, keys, values = tuple(result)
    query = query.astype(jnp.bfloat16).reshape(seg, heads, hsize)
    keys = keys.astype(jnp.bfloat16).reshape(seg, heads, hsize)
    values = values.astype(jnp.bfloat16).reshape(seg, heads, hsize)
    fkey = feature(keys.astype(jnp.float32)).astype(jnp.bfloat16)
    mem_term = jnp.einsum("thd,the->hde", fkey, values, preferred_element_type=jnp.float32)
    norm_term = jnp.sum(fkey.astype(jnp.float32), axis=0)
    zeros_pair = (jnp.zeros_like(mem_term), jnp.zeros_like(norm_term))
    memory, normal = carried_in((mem_term, norm_term), SEQ, add_pairs, zeros_pair)
    rows = lax.broadcasted_iota(jnp.int32, (seg, seg), 0)
    cols = lax.broadcasted_iota(jnp.int32, (seg, seg), 1)
    causal = cols <= rows
    scale = 1.0 / hsize**0.5
    scores = jnp.einsum("qhd,khd->hqk", query, keys, preferred_element_type=jnp.float32) * scale
    scores = jnp.where(causal[None], scores, -1e30)
    expo = jnp.exp(scores - jnp.max(scores, axis=2, keepdims=True))
    probs = (expo / jnp.sum(expo, axis=2, keepdims=True)).astype(jnp.bfloat16)
    local = jnp.einsum("hqk,khd->qhd", probs, values, preferred_element_type=jnp.float32)
    fquery = feature(query.astype(jnp.float32)).astype(jnp.bfloat16).astype(jnp.float32)
    numer = jnp.einsum("thd,hde->the", fquery, memory, precision=lax.Precision.HIGHEST)
    denom = jnp.einsum("thd,hd->th", fquery, normal, precision=lax.Precision.HIGHEST)
    readout = numer / jnp.maximum(denom, 1.0)[:, :, None]
    share = jax.nn.sigmoid(mix_logit)[None, :, None]
    mixed = (share * readout + (1.0 - share) * local).astype(jnp.bfloat16).reshape(seg, width)
    columns = lax.all_to_all(w_out, "head", split_axis=1, concat_axis=0, tiled=True)
    summed = jnp.dot(
        lax.all_gather(mixed, "head", axis=1, tiled=True),
        columns,
        preferred_element_type=jnp.float32,
    )
    return summed.astype(jnp.bfloat16)


def solution(mesh):
    torus = Mesh(
        mesh.devices.reshape(8, 4, 2, mesh.shape["head"]), ("seq_0", "seq_1", "seq_2", "head")
    )
    return jax.shard_map(
        on_device,
        mesh=torus,
        in_specs=(
            P(SEQ, "head"),
            P(None, "head"),
            P(None, "head"),
            P(None, "head"),
            P("head", None),
            P("head"),
        ),
        out_specs=P(SEQ, "head"),
        check_vma=False,
    )
```

profile of v0, /device:TPU:1, one launch (start us, length us, event | category | flops | bytes accessed | tf_op | source)
XLA Modules:
  0.0 251.1 jit_solution(9462103053753191697)
XLA Ops:
  6.5 0.0 copy-start
  6.5 0.0 all-gather.6.cloned.1.call-start
  6.5 0.7 all-gather.6.cloned.1.call-update
  7.3 0.0 all-gather.8.cloned.1.call-start
  7.3 56.3 %all-gather.6.cloned.1.call-done = bf16[1024,2048]{1,0:T(8,128)(2,1)} async-done(((bf16[1024,512]{1,0:T(8,128)(2,1)}), bf16[1024,2048]{1,0:T(8,128)(2,1)}) %all-gather.6.cloned.1.call-update) | async-done | bytes 4194320 | tf_op jit(solution)/shard_map/all_gather | solution.py:52
  63.6 0.0 copy-done
  63.6 6.2 %fusion.20 = (bf16[512]{0:T(512)(128)(2,1)S(1)}, bf16[1024,512]{0,1:T(8,128)(2,1)}) fusion(bf16[1024,2048]{1,0:T(8,128)(2,1)} %all-gather.6.cloned.1.call-done, bf16[2048,512]{1,0:T(8,128)(2,1)S(1)} %copy-done), kind=kOutput, calls=%fused_computation.36 | convolution fusion | flops 2151677440 | bytes 7341056 | tf_op jit(solution)/shard_map/dot_general | solution.py:55
  69.8 2.3 copy.33
  72.1 0.0 copy-start.1
  72.1 5.3 %convolution_convert_fusion.2 = bf16[1024,512]{0,1:T(8,128)(2,1)S(1)} fusion(bf16[1024,2048]{1,0:T(8,128)(2,1)} %all-gather.6.cloned.1.call-done, bf16[2048,512]{1,0:T(8,128)(2,1)} %param.9), kind=kOutput, calls=%fused_computation.31 | convolution fusion | flops 2148007936 | bytes 7340032 | tf_op jit(solution)/shard_map/dot_general | solution.py:55
  77.4 0.0 copy-start.3
  77.4 0.0 copy-done.1
  77.4 0.0 copy-start.2
  77.4 1.2 convolution_convert_fusion.4
  78.7 0.0 copy-done.3
  78.7 2.7 %all-gather = bf16[4,256,256]{2,1,0:T(8,128)(2,1)S(1)} all-gather(bf16[2,256,256]{2,1,0:T(8,128)(2,1)S(1)} %convolution_convert_fusion.4), channel_id=2, replica_groups=mesh['seq_0'=8,'seq_1'=4,'seq_2'=2,'head'=4] {'seq_2'}, dimensions={0}, use_global_device_ids=true | all-gather | bytes 786432 | tf_op jit(solution)/shard_map/all_gather | solution.py:22
  81.3 0.8 fusion.59
  82.1 0.0 all-gather.8.cloned.1.call-update
  82.1 0.0 all-gather.10.cloned.1.call-start
  82.2 0.0 copy-done.2
  82.2 24.7 %all-gather.8.cloned.1.call-done = bf16[4,2,256,256]{3,2,1,0:T(8,128)(2,1)} async-done(((bf16[1,2,256,256]{3,2,1,0:T(8,128)(2,1)}), bf16[4,2,256,256]{3,2,1,0:T(8,128)(2,1)}) %all-gather.8.cloned.1.call-update) | async-done | bytes 1048592 | tf_op jit(solution)/shard_map/all_gather | solution.py:22
  106.9 2.0 fusion.55
  108.9 0.0 all-gather.10.cloned.1.call-update
  108.9 0.0 all-gather.12.cloned.1.call-start
  109.0 1.3 iota_compare_fusion
  110.3 6.2 %convolution_convert_fusion.1 = bf16[1024,512]{0,1:T(8,128)(2,1)} fusion(bf16[1024,2048]{1,0:T(8,128)(2,1)} %all-gather.6.cloned.1.call-done, bf16[2048,512]{1,0:T(8,128)(2,1)} %param.7), kind=kOutput, calls=%fused_computation.30 | convolution fusion | flops 2148007936 | bytes 7340032 | tf_op jit(solution)/shard_map/dot_general | solution.py:55
  116.5 2.3 copy.36
  118.8 4.2 %all_gather.40 = bf16[2,2,256]{2,1,0:T(2,128)(2,1)S(1)} all-gather(bf16[1,2,256]{2,1,0:T(2,128)(2,1)S(1)} %all_gather.39), channel_id=1, replica_groups=mesh['seq_0'=8,'seq_1'=4,'seq_2'=2,'head'=4] {'seq_2'}, dimensions={0}, use_global_device_ids=true | all-gather | bytes 3072 | tf_op jit(solution)/shard_map/all_gather | solution.py:22
  123.0 6.7 %all_gather.41 = bf16[4,2,256]{2,1,0:T(2,128)(2,1)S(1)} all-gather(bf16[1,2,256]{2,1,0:T(2,128)(2,1)S(1)} %fusion.106), channel_id=1, replica_groups=mesh['seq_0'=8,'seq_1'=4,'seq_2'=2,'head'=4] {'seq_1'}, dimensions={0}, use_global_device_ids=true | all-gather | bytes 5120 | tf_op jit(solution)/shard_map/all_gather | solution.py:22
  129.7 14.9 %all_gather.42 = bf16[8,2,256]{2,1,0:T(2,128)(2,1)S(1)} all-gather(bf16[1,2,256]{2,1,0:T(2,128)(2,1)S(1)} %fusion.105), channel_id=1, replica_groups=mesh['seq_0'=8,'seq_1'=4,'seq_2'=2,'head'=4] {'seq_0'}, dimensions={0}, use_global_device_ids=true | all-gather | bytes 9216 | tf_op jit(solution)/shard_map/all_gather | solution.py:22
  144.6 2.8 %fusion.56 = f32[2,1,1024]{2,1,0:T(1,128)S(1)} fusion(bf16[1024,2,256]{2,0,1:T(8,128)(2,1)} %copy.36, f32[2,256,1]{1,0,2:T(2,128)S(1)} %fusion.94), kind=kOutput, calls=%fused_computation.76 | convolution fusion | flops 9437184 | bytes 1058816 | tf_op jit(solution)/shard_map/thd,hd->th/dot_general | solution.py:76
  147.4 8.4 %fusion.115 = (f32[2,1024]{1,0:T(2,128)S(1)}, f32[2,1024,1024]{1,2,0:T(8,128)}) fusion(pred[1024,1024]{0,1:T(8,128)(4,1)} %iota_compare_fusion, bf16[1024,2,256]{0,2,1:T(8,128)(2,1)} %bitcast.57, bf16[1024,2,256]{0,2,1:T(8,128)(2,1)} %bitcast.54), kind=kOutput, calls=%fused_computation.145 | convolution fusion | flops 1082131456 | bytes 11542528 | tf_op jit(solution)/shard_map/sub | solution.py:71
  155.8 6.3 %fusion.4 = f32[2,256,1024]{2,1,0:T(8,128)} fusion(bf16[1024,2,256]{0,2,1:T(8,128)(2,1)} %bitcast.59, f32[2,1024,1024]{1,2,0:T(8,128)} %get-tuple-element.8, f32[2,1024]{1,0:T(2,128)S(1)} %get-tuple-element.7), kind=kOutput, calls=%fused_computation.14 | convolution fusion | flops 1077936128 | bytes 11542528 | tf_op jit(solution)/shard_map/hqk,khd->qhd/dot_general | solution.py:73
  162.1 0.0 all-gather.10.cloned.1.call-done
  162.1 7.4 %fusion.15 = bf16[1024,2,256]{0,2,1:T(8,128)(2,1)} fusion(f32[2,256,1024]{2,1,0:T(8,128)} %fusion.4, f32[2]{0:T(128)S(1)} %get-tuple-element.5, f32[1024,2]{0,1:T(2,128)S(1)} %fusion.90, f32[2]{0:T(128)S(1)} %get-tuple-element.6, bf16[1024,2,256]{2,0,1:T(8,128)(2,1)} %copy.36, bf16[8,2,256,256]{3,2,1,0:T(8,128)(2,1)} %all-gather.10.cloned.1.call-done, ...), kind=kOutput, calls=%fused_computation.26 | convolution fusion | flops 1621753856 | bytes 7872542 | tf_op jit(solution)/shard_map/thd,hde->the/dot_general | solution.py:75
  169.5 0.0 all-gather.12.cloned.1.call-update
  169.5 4.0 %copy.41 = bf16[512,2048]{0,1:T(8,128)(2,1)} copy(bf16[512,2048]{1,0:T(8,128)(2,1)} %param.10) | data formatting | bytes 4194304 | tf_op args[4]
  173.5 39.7 %all_to_all.19 = bf16[512,4,512]{0,2,1:T(8,128)(2,1)} all-to-all(bf16[512,4,512]{0,2,1:T(8,128)(2,1)} %bitcast.51), channel_id=1, replica_groups=mesh['seq_0'=8,'seq_1'=4,'seq_2'=2,'head'=4] {'head'}, dimensions={1} | all-to-all | bytes 4194304 | tf_op jit(solution)/shard_map/all_to_all | solution.py:80
  213.2 4.2 %copy.42 = bf16[4,512,512]{2,1,0:T(8,128)(2,1)} copy(bf16[4,512,512]{1,2,0:T(8,128)(2,1)} %bitcast.50) | data formatting | bytes 4194304 | tf_op jit(solution)/shard_map/all_to_all | solution.py:80
  217.4 21.0 %all-gather.12.cloned.1.call-done = bf16[1024,2048]{0,1:T(8,128)(2,1)} async-done(((bf16[1024,512]{0,1:T(8,128)(2,1)}), bf16[1024,2048]{0,1:T(8,128)(2,1)}) %all-gather.12.cloned.1.call-update) | async-done | bytes 4194320 | tf_op jit(solution)/shard_map/all_gather | solution.py:82
  238.4 6.2 %convolution_convert_fusion = bf16[1024,512]{1,0:T(8,128)(2,1)} fusion(bf16[1024,2048]{0,1:T(8,128)(2,1)} %all-gather.12.cloned.1.call-done, bf16[2048,512]{1,0:T(8,128)(2,1)} %bitcast.52), kind=kOutput, calls=%fused_computation.29 | convolution fusion | flops 2148007936 | bytes 7340032 | tf_op jit(solution)/shard_map/dot_general | solution.py:81
  (6 shorter events, 0.1 us)
Async XLA Ops:
  6.5 57.0 %copy-start = (bf16[2048,512]{1,0:T(8,128)(2,1)S(1)}, bf16[2048,512]{1,0:T(8,128)(2,1)}, u32[]{:S(2)}) copy-start(bf16[2048,512]{1,0:T(8,128)(2,1)} %param.8) | copy-start | bytes 6291460
  6.5 57.0 %all-gather.6.cloned.1.call-start = ((), (), s32[]{:S(2)}) async-start(), calls=%async_computation.1 | async-start | bytes 5242880 | tf_op jit(solution)/shard_map/all_gather | solution.py:52
  7.3 99.6 %all-gather.8.cloned.1.call-start = ((), (), s32[]{:S(2)}) async-start(), calls=%async_computation.2 | async-start | bytes 1310720 | tf_op jit(solution)/shard_map/all_gather | solution.py:22
  72.1 5.3 %copy-start.1 = (bf16[1024,2,256]{2,0,1:T(8,128)(2,1)S(1)}, bf16[1024,2,256]{2,0,1:T(8,128)(2,1)}, u32[]{:S(2)}) copy-start(bf16[1024,2,256]{2,0,1:T(8,128)(2,1)} %copy.33) | copy-start | bytes 3145732
  77.4 1.3 copy-start.3
  77.4 4.8 %copy-start.2 = (f32[2]{0:T(128)S(1)}, f32[2]{0:T(128)}, u32[]{:S(2)}) copy-start(f32[2]{0:T(128)} %param.11) | copy-start | bytes 28
  82.1 80.0 %all-gather.10.cloned.1.call-start = ((), (), s32[]{:S(2)}) async-start(), calls=%async_computation.3 | async-start | bytes 2359296 | tf_op jit(solution)/shard_map/all_gather | solution.py:22
  108.9 129.4 %all-gather.12.cloned.1.call-start = ((), (), s32[]{:S(2)}) async-start(), calls=%async_computation.4 | async-start | bytes 5242880 | tf_op jit(solution)/shard_map/all_gather | solution.py:82
Sparse Core Ops, SparseCore 0:
  9.1 54.3 all-gather.5
  82.2 24.5 all-gather.7
  109.0 39.1 all-gather.9
  169.6 68.6 all-gather.11
where the time goes:
time: 252 us; the launch traced here: 251 us
  waiting for transfers between devices  103 us (41%)
  blocking collectives  68.1 us (27%)
  matrix products  50.1 us (20%)
  between operations  13.2 us (5%)
  local copies, waits for them, and re-layouts  12.8 us (5%)
  other arithmetic  4.18 us (2%)
    all_gather x1, waiting for transfers between devices, on_device(): piece = lax.all_gather(tokens, 'head', axis=1, tiled=True)  56.3 us
    all_to_all x1, blocking collectives, on_device(): lax.all_to_all(w_out, 'head', split_axis=1, concat_axis=0, tiled=True)  39.7 us
    all_gather x4, blocking collectives, carried_in(): lax.all_gather(part.astype(kind), axis)  28.4 us
    all_gather x2, waiting for transfers between devices, carried_in(): lax.all_gather(part.astype(kind), axis)  24.7 us
    all_gather x1, waiting for transfers between devices, on_device(): lax.all_gather(mixed, 'head', axis=1, tiled=True)  21 us
    dot_general x3, matrix products, on_device(): result.append(jnp.dot(piece, weight, preferred_element_type=jnp.float32))  17.7 us
    sub x1, matrix products, on_device(): expo = jnp.exp(scores - jnp.max(scores, axis=2, keepdims=True))  8.38 us
    dot_general x1, matrix products, on_device(): jnp.einsum('thd,hde->the', fquery, memory, precision=lax.Precision.HIGHEST)  7.36 us
  transfers between devices with their start and end apart: 4, of which 3 were waited for; matrix products, arithmetic and copies ran while one was open for 14% of the time, Pallas kernels for 0%

commit v1 on v0

v1 whole, which is shorter than its diff:
```python
import functools

import jax
import jax.numpy as jnp
from jax import lax
from jax.experimental import pallas as pl
from jax.experimental.pallas import tpu as pltpu
from jax.sharding import Mesh
from jax.sharding import PartitionSpec as P

SEQ = ("z", "x", "c")
MESH = pl.DeviceIdType.MESH
F32, BF16 = jnp.float32, jnp.bfloat16
NZ, NX, NC, NY = 8, 4, 2, 4
NE = NX * NC
NU = 2
ZORDER = (1, 7, 2, 6, 3, 5, 4)
NT = (((1,), (1,)), ((), ()))
TN = (((0,), (0,)), ((), ()))


def feature(values):
    return jnp.where(values > 0, values + 1.0, jnp.exp(values))


def kernel(
    tok, wq, wk, wv, wo, logit, out,
    xbuf, wbuf, acc, q_s, k_s, v_s, loc, wof, macc, nacc, mt, ga, tb, gb, pc, gc, mem, mixs, mixr, outs,
    lsem, tsend, trecv, w0s, w0r, w1s, w1r, w2s, w2r, w3s, w3r, asend, arecv, bsend, brecv, csend, crecv,
    msend, mrecv, osend, orecv,
):
    z, x, c, y = (lax.axis_index(a) for a in ("z", "x", "c", "y"))
    e = x * NC + c
    seg, fs = tok.shape
    heads, _, hs = q_s.shape
    rc = seg // 4
    gw = heads * hs
    pr = heads * hs // NE
    br = gw // (NZ * NX)
    half = wo.shape[1] // NC
    rem = lax.rem

    def yy(r):
        return {"y": rem(y + r, NY)}

    def zz(d):
        return {"z": rem(z + d, NZ)}

    def xx(i):
        return {"x": rem(x + i, NX)}

    def ee(i):
        o = rem(e + i, NE)
        return {"x": lax.div(o, NC), "c": rem(o, NC)}

    def remote(src, dst, ssem, rsem, dev):
        return pltpu.make_async_remote_copy(
            src_ref=src, dst_ref=dst, send_sem=ssem, recv_sem=rsem, device_id=dev, device_id_type=MESH
        )

    local = []

    def fetch(src, dst):
        cp = pltpu.make_async_copy(src, dst, lsem.at[len(local)])
        cp.start()
        local.append(cp)

    fetch(tok, xbuf.at[0])
    for r in range(NY):
        rows = pl.ds(pl.multiple_of(rem(y + r, NY) * fs, fs), fs)
        for i, w in enumerate((wk, wv, wq)):
            fetch(w.at[rows, :], wbuf.at[r, :, pl.ds(i * gw, gw)])
    fetch(wo, wof.at[0])

    barrier = pltpu.get_barrier_semaphore()
    peers = [yy(r) for r in range(1, NY)] + [ee(i) for i in range(1, NE)] + [zz(d) for d in range(1, NZ)]
    for dev in peers:
        pl.semaphore_signal(barrier, inc=1, device_id=dev, device_id_type=MESH)
    pl.semaphore_wait(barrier, len(peers))

    def chunk(j):
        return pl.ds(pl.multiple_of(j * rc, rc), rc)

    def t_own(j, way):
        rows = chunk(j if way == 0 else 3 - j)
        return remote(
            tok.at[rows, :], xbuf.at[3 if way == 0 else 1, rows, :],
            tsend.at[way, j], trecv.at[way, j], yy(1 if way == 0 else 3),
        )

    def t_far(j, way):
        rows = chunk(j if way == 0 else 3 - j)
        return remote(
            xbuf.at[3 if way == 0 else 1, rows, :], xbuf.at[2, rows, :],
            tsend.at[way, 4 + j], trecv.at[way, 4 + j], yy(1 if way == 0 else 3),
        )

    cols = pl.ds(pl.multiple_of(c * half, half), half)

    def piece(xp, zp):
        return pl.ds(pl.multiple_of((xp * NZ + zp) * br, br), br)

    def w_y(r):
        return remote(wo.at[piece(x, z), cols], wof.at[NY - r, piece(x, z), cols], w0s.at[r], w0r.at[r], yy(r))

    def w_z(d):
        ref = wof.at[pl.ds(1, NY - 1), piece(x, z), cols]
        return remote(ref, ref, w1s.at[d], w1r.at[d], zz(d))

    def w_x(i, d):
        ref = wof.at[pl.ds(1, NY - 1), piece(x, rem(z + NZ - d, NZ)), cols]
        return remote(ref, ref, w2s.at[i, d], w2r.at[i, d], xx(i))

    def w_c():
        ref = wof.at[pl.ds(1, NY - 1), :, cols]
        return remote(ref, ref, w3s.at[0], w3r.at[0], {"c": 1 - c})

    for r in range(1, NY):
        w_y(r).start()
    for j in range(4):
        t_own(j, 0).start()
        t_own(j, 1).start()

    for cp in local:
        cp.wait()
    macc[...] = jnp.zeros_like(macc)
    nacc[...] = jnp.zeros_like(nacc)
    mt[...] = jnp.zeros_like(mt)

    def own_dot(j, carry):
        rows = chunk(j)
        acc[rows, :] = jnp.dot(xbuf[0, rows, :], wbuf[0], preferred_element_type=F32)
        return carry

    lax.fori_loop(0, 4, own_dot, 0)

    for r in range(1, NY):
        w_y(r).wait_recv()
    for d in ZORDER:
        w_z(d).start()
    for i in range(1, NX):
        w_x(i, 0).start()

    def w_forward(d):
        w_z(d).wait_recv()
        for i in range(1, NX):
            w_x(i, d).start()

    def ring_dot(j, way):
        rows = chunk(j if way == 0 else 3 - j)
        slot = 3 if way == 0 else 1
        acc[rows, :] += jnp.dot(xbuf[slot, rows, :], wbuf[slot], preferred_element_type=F32)

    forward_at = {0: (1, 7), 1: (2, 6), 2: (3, 5), 3: (4,)}
    for j in range(4):
        for way in range(2):
            t_own(j, way).wait_recv()
            if j < 2:
                t_far(j, way).start()
        for d in forward_at[j]:
            w_forward(d)
        for way in range(2):
            ring_dot(j, way)

    def far_rows(rows):
        kv = acc[rows, 0 : 2 * gw] + jnp.dot(xbuf[2, rows, :], wbuf[2, :, 0 : 2 * gw], preferred_element_type=F32)
        kv = kv.astype(BF16)
        for h in range(heads):
            key = kv[:, h * hs : (h + 1) * hs]
            val = kv[:, gw + h * hs : gw + (h + 1) * hs]
            k_s[h, rows, :] = key
            v_s[h, rows, :] = val
            fk = feature(key.astype(F32)).astype(BF16)
            macc[h] += lax.dot_general(fk, val, TN, preferred_element_type=F32)
            nacc[h] += jnp.sum(fk.astype(F32).reshape(rc // 8, 8, hs), axis=0)

    for j in range(2):
        for way in range(2):
            t_far(j, way).wait_recv()
        for way in range(2):
            far_rows(chunk(j if way == 0 else 3 - j))

    per_head = hs // pr
    for h in range(heads):
        norm = jnp.sum(nacc[h], axis=0, keepdims=True)
        norm_rows = jnp.where(lax.broadcasted_iota(jnp.int32, (16, hs), 0) == h, norm, 0.0)
        for p in range(NE):
            if p // per_head == h:
                mt[p, 0:pr, :] = macc[h, (p % per_head) * pr : (p % per_head + 1) * pr, :].astype(BF16)
            mt[p, pr : pr + 16, :] += norm_rows.astype(BF16)

    def a_copy(i):
        return remote(mt.at[rem(e + i, NE)], ga.at[e], asend.at[i], arecv.at[i], ee(i))

    def b_copy(d):
        return remote(tb, gb.at[z], bsend.at[d], brecv.at[d], zz(d))

    def c_copy(i):
        return remote(pc.at[rem(e + i, NE)], gc.at[e], csend.at[i], crecv.at[i], ee(i))

    for i in range(1, NE):
        a_copy(i).start()
    ga[e] = mt[e]

    def q_rows(j, carry):
        rows = chunk(j)
        q = acc[rows, 2 * gw : 3 * gw] + jnp.dot(
            xbuf[2, rows, :], wbuf[2, :, 2 * gw : 3 * gw], preferred_element_type=F32
        )
        q = q.astype(BF16)
        for h in range(heads):
            q_s[h, rows, :] = q[:, h * hs : (h + 1) * hs]
        return carry

    lax.fori_loop(0, 4, q_rows, 0)

    shares = [jax.nn.sigmoid(jnp.full((1, hs), logit[h], F32)) for h in range(heads)]
    scale = 1.0 / hs**0.5
    lower = lax.broadcasted_iota(jnp.int32, (rc, rc), 1) <= lax.broadcasted_iota(jnp.int32, (rc, rc), 0)

    def attend(h):
        for i in range(4):
            rows = slice(i * rc, (i + 1) * rc)
            q = q_s[h, rows, :]
            diag = lax.dot_general(q, k_s[h, rows, :], NT, preferred_element_type=F32) * scale
            diag = jnp.where(lower, diag, -1e30)
            top = jnp.max(diag, axis=1, keepdims=True)
            if i:
                before = lax.dot_general(q, k_s[h, 0 : i * rc, :], NT, preferred_element_type=F32) * scale
                top = jnp.maximum(top, jnp.max(before, axis=1, keepdims=True))
                pb = jnp.exp(before - top)
            pd = jnp.exp(diag - top)
            total = jnp.sum(pd, axis=1, keepdims=True)
            got = jnp.dot(pd.astype(BF16), v_s[h, rows, :], preferred_element_type=F32)
            if i:
                total += jnp.sum(pb, axis=1, keepdims=True)
                got += jnp.dot(pb.astype(BF16), v_s[h, 0 : i * rc, :], preferred_element_type=F32)
            loc[h, rows, :] = got / total * (1.0 - shares[h])

    attend(0)

    for i in range(1, NE):
        a_copy(i).wait_recv()
    plane = ga[0].astype(F32)
    for p in range(1, NE):
        plane += ga[p].astype(F32)
    tb[...] = plane.astype(BF16)
    for d in range(1, NZ):

        @pl.when(z + d < NZ)
        def _(d=d):
            b_copy(d).start()

    attend(1)

    for d in range(1, NZ):

        @pl.when(z - d >= 0)
        def _(d=d):
            b_copy(d).wait_recv()

    run = lax.fori_loop(0, z, lambda k, s: s + gb[k].astype(F32), jnp.zeros(tb.shape, F32))
    for p in range(NE):
        pc[p] = run.astype(BF16)
        run += ga[p].astype(F32)
    for i in range(1, NE):
        c_copy(i).start()
    gc[e] = pc[e]

    for i in range(1, NX):
        for d in range(NZ):
            w_x(i, d).wait_recv()
    w_c().start()

    for i in range(1, NE):
        c_copy(i).wait_recv()
    for p in range(NE):
        mem[p // per_head, (p % per_head) * pr : (p % per_head + 1) * pr, :] = gc[p, 0:pr, :]

    sub = rc // NU

    def m_copy(r, u):
        rows = pl.ds(u * sub, sub)
        return remote(mixs.at[r, rows, :], mixr.at[NY - r, rows, :], msend.at[r, u], mrecv.at[r, u], yy(r))

    def mix(r):
        base = rem(y + r, NY) * rc
        for u in range(NU):
            rows = pl.ds(pl.multiple_of(base + u * sub, sub), sub)
            for h in range(heads):
                fq = feature(q_s[h, rows, :].astype(F32)).astype(BF16)
                norm = jnp.broadcast_to(gc[0, pr + h : pr + h + 1, :], (hs, hs))
                denom = lax.dot_general(fq, norm, NT, preferred_element_type=F32)
                numer = jnp.dot(fq, mem[h], preferred_element_type=F32)
                val = shares[h] * (numer / jnp.maximum(denom, 1.0)) + loc[h, rows, :]
                dst = mixs if r else mixr
                dst[r, u * sub : (u + 1) * sub, h * hs : (h + 1) * hs] = val.astype(BF16)
            if r:
                m_copy(r, u).start()

    for r in (2, 1, 3, 0):
        mix(r)

    w_c().wait_recv()

    def o_copy(r, u):
        rows = pl.ds(pl.multiple_of(y * rc + u * sub, sub), sub)
        return remote(outs.at[r, pl.ds(u * sub, sub), :], out.at[rows, :], osend.at[r, u], orecv.at[r, u], yy(r))

    keep = []
    for u in range(NU):
        rows = slice(u * sub, (u + 1) * sub)
        for r in range(1, NY):
            m_copy(r, u).wait_recv()
        for r in (2, 1, 3, 0):
            oc = pl.ds(pl.multiple_of(rem(y + r, NY) * fs, fs), fs)
            o = jnp.dot(mixr[0, rows, :], wof[0, :, oc], preferred_element_type=F32)
            for s in range(1, NY):
                o += jnp.dot(mixr[s, rows, :], wof[s, :, oc], preferred_element_type=F32)
            outs[r, rows, :] = o.astype(BF16)
            if r:
                o_copy(r, u).start()
            else:
                orows = pl.ds(pl.multiple_of(y * rc + u * sub, sub), sub)
                cp = pltpu.make_async_copy(outs.at[0, pl.ds(u * sub, sub), :], out.at[orows, :], lsem.at[u])
                cp.start()
                keep.append(cp)

    for cp in keep:
        cp.wait()
    for u in range(NU):
        for r in range(1, NY):
            o_copy(r, u).wait_recv()
    for u in range(NU):
        for r in range(1, NY):
            o_copy(r, u).wait_send()
            m_copy(r, u).wait_send()
    for way in range(2):
        for j in range(4):
            t_own(j, way).wait_send()
        for j in range(2):
            t_far(j, way).wait_send()
    for r in range(1, NY):
        w_y(r).wait_send()
    for d in range(1, NZ):
        w_z(d).wait_send()
    for i in range(1, NX):
        for d in range(NZ):
            w_x(i, d).wait_send()
    w_c().wait_send()
    for i in range(1, NE):
        a_copy(i).wait_send()
        c_copy(i).wait_send()
    for d in range(1, NZ):

        @pl.when(z + d < NZ)
        def _(d=d):
            b_copy(d).wait_send()


def on_device(tokens, w_query, w_key, w_value, w_out, mix_logit):
    seg, fs = tokens.shape
    heads = mix_logit.shape[0]
    gw = w_query.shape[1]
    hs = gw // heads
    pr = heads * hs // NE
    rc = seg // 4
    width = w_out.shape[1]
    hbm = pl.BlockSpec(memory_space=pl.ANY)
    dma = pltpu.SemaphoreType.DMA
    return pl.pallas_call(
        kernel,
        out_shape=jax.ShapeDtypeStruct((seg, fs), BF16),
        in_specs=[hbm] * 5 + [pl.BlockSpec(memory_space=pltpu.SMEM)],
        out_specs=hbm,
        scratch_shapes=[
            pltpu.VMEM((NY, seg, fs), BF16),
            pltpu.VMEM((NY, fs, 3 * gw), BF16),
            pltpu.VMEM((seg, 3 * gw), F32),
            pltpu.VMEM((heads, seg, hs), BF16),
            pltpu.VMEM((heads, seg, hs), BF16),
            pltpu.VMEM((heads, seg, hs), BF16),
            pltpu.VMEM((heads, seg, hs), F32),
            pltpu.VMEM((NY, gw, width), BF16),
            pltpu.VMEM((heads, hs, hs), F32),
            pltpu.VMEM((heads, 8, hs), F32),
            pltpu.VMEM((NE, pr + 16, hs), BF16),
            pltpu.VMEM((NE, pr + 16, hs), BF16),
            pltpu.VMEM((pr + 16, hs), BF16),
            pltpu.VMEM((NZ, pr + 16, hs), BF16),
            pltpu.VMEM((NE, pr + 16, hs), BF16),
            pltpu.VMEM((NE, pr + 16, hs), BF16),
            pltpu.VMEM((heads, hs, hs), BF16),
            pltpu.VMEM((NY, rc, gw), BF16),
            pltpu.VMEM((NY, rc, gw), BF16),
            pltpu.VMEM((NY, rc, fs), BF16),
            dma((14,)),
            dma((2, 6)), dma((2, 6)),
            dma((NY,)), dma((NY,)),
            dma((NZ,)), dma((NZ,)),
            dma((NX, NZ)), dma((NX, NZ)),
            dma((1,)), dma((1,)),
            dma((NE,)), dma((NE,)),
            dma((NZ,)), dma((NZ,)),
            dma((NE,)), dma((NE,)),
            dma((NY, NU)), dma((NY, NU)),
            dma((NY, NU)), dma((NY, NU)),
        ],
        compiler_params=pltpu.CompilerParams(
            collective_id=0, has_side_effects=True, vmem_limit_bytes=60 * 2**20
        ),
    )(tokens, w_query, w_key, w_value, w_out, mix_logit)


def solution(mesh):
    torus = Mesh(mesh.devices.reshape(NZ, NX, NC, NY), ("z", "x", "c", "y"))
    return jax.shard_map(
        on_device,
        mesh=torus,
        in_specs=(P(SEQ, "y"), P(None, "y"), P(None, "y"), P(None, "y"), P("y", None), P("y")),
        out_specs=P(SEQ, "y"),
        check_vma=False,
    )
```

time: 252 us -> 96.5 us (0.38)
  the two profiles are of different devices: /device:TPU:1 before, /device:TPU:193 now
where the time goes in v1:
time: 96.5 us; the launch traced here: 96.4 us
  Pallas kernels  94.1 us (98%)
  local copies, waits for them, and re-layouts  2.26 us (2%)
    pallas_call x1, Pallas kernels, on_device(): pl.pallas_call(kernel, out_shape=jax.ShapeDtypeStruct((seg, fs), BF16), i...  94.1 us
    unnamed x1, local copies, waits for them, and re-layouts  2.26 us

profile of v1, /device:TPU:193, one launch (start us, length us, event | category | flops | bytes accessed | tf_op | source)
XLA Modules:
  0.0 96.4 jit_solution(10832938560608787675)
XLA Ops:
  0.0 94.1 %shard_map.64 = bf16[1024,512]{1,0:T(8,128)(2,1)} custom-call(bf16[1024,512]{1,0:T(8,128)(2,1)} %tok.1, bf16[2048,512]{1,0:T(8,128)(2,1)} %wq.1, bf16[2048,512]{1,0:T(8,128)(2,1)} %wk.1, bf16[2048,512]{1,0:T(8,128)(2,1)} %wv.1, bf16[512,2048]{1,0:T(8,128)(2,1)} %wo.1, f32[2]{0:T(128)} %logit.1), custom_call_target="tpu_custom_call" | custom-call | tf_op jit(solution)/shard_map/pallas_call | solution.py:371
  94.1 2.3 %copy.8 = bf16[1024,512]{1,0:T(8,128)(2,1)} copy(bf16[1024,512]{1,0:T(8,128)(2,1)} %shard_map.64) | data formatting | bytes 2097152

commit v2 on v1

--- a/solution.py
+++ b/solution.py
@@ -58,19 +58,18 @@
             src_ref=src, dst_ref=dst, send_sem=ssem, recv_sem=rsem, device_id=dev, device_id_type=MESH
         )
 
-    local = []
-
-    def fetch(src, dst):
-        cp = pltpu.make_async_copy(src, dst, lsem.at[len(local)])
-        cp.start()
-        local.append(cp)
-
-    fetch(tok, xbuf.at[0])
+    def fetch(src, dst, k):
+        pltpu.make_async_copy(src, dst, lsem.at[k]).start()
+
+    def done(ref, sem):
+        pltpu.make_async_copy(ref, ref, sem).wait()
+
+    fetch(tok, xbuf.at[0], 0)
     for r in range(NY):
         rows = pl.ds(pl.multiple_of(rem(y + r, NY) * fs, fs), fs)
         for i, w in enumerate((wk, wv, wq)):
-            fetch(w.at[rows, :], wbuf.at[r, :, pl.ds(i * gw, gw)])
-    fetch(wo, wof.at[0])
+            fetch(w.at[rows, :], wbuf.at[r, :, pl.ds(i * gw, gw)], 1)
+    fetch(wo, wof.at[0], 2)
 
     barrier = pltpu.get_barrier_semaphore()
     peers = [yy(r) for r in range(1, NY)] + [ee(i) for i in range(1, NE)] + [zz(d) for d in range(1, NZ)]
@@ -85,14 +84,14 @@
         rows = chunk(j if way == 0 else 3 - j)
         return remote(
             tok.at[rows, :], xbuf.at[3 if way == 0 else 1, rows, :],
-            tsend.at[way, j], trecv.at[way, j], yy(1 if way == 0 else 3),
+            tsend.at[0], trecv.at[way, j], yy(1 if way == 0 else 3),
         )
 
     def t_far(j, way):
         rows = chunk(j if way == 0 else 3 - j)
         return remote(
             xbuf.at[3 if way == 0 else 1, rows, :], xbuf.at[2, rows, :],
-            tsend.at[way, 4 + j], trecv.at[way, 4 + j], yy(1 if way == 0 else 3),
+            tsend.at[0], trecv.at[way, 4 + j], yy(1 if way == 0 else 3),
         )
 
     cols = pl.ds(pl.multiple_of(c * half, half), half)
@@ -101,15 +100,15 @@
         return pl.ds(pl.multiple_of((xp * NZ + zp) * br, br), br)
 
     def w_y(r):
-        return remote(wo.at[piece(x, z), cols], wof.at[NY - r, piece(x, z), cols], w0s.at[r], w0r.at[r], yy(r))
+        return remote(wo.at[piece(x, z), cols], wof.at[NY - r, piece(x, z), cols], w0s.at[0], w0r.at[0], yy(r))
 
     def w_z(d):
         ref = wof.at[pl.ds(1, NY - 1), piece(x, z), cols]
-        return remote(ref, ref, w1s.at[d], w1r.at[d], zz(d))
+        return remote(ref, ref, w1s.at[0], w1r.at[d], zz(d))
 
     def w_x(i, d):
         ref = wof.at[pl.ds(1, NY - 1), piece(x, rem(z + NZ - d, NZ)), cols]
-        return remote(ref, ref, w2s.at[i, d], w2r.at[i, d], xx(i))
+        return remote(ref, ref, w2s.at[0], w2r.at[0], xx(i))
 
     def w_c():
         ref = wof.at[pl.ds(1, NY - 1), :, cols]
@@ -121,8 +120,8 @@
         t_own(j, 0).start()
         t_own(j, 1).start()
 
-    for cp in local:
-        cp.wait()
+    done(xbuf.at[0], lsem.at[0])
+    done(wbuf, lsem.at[1])
     macc[...] = jnp.zeros_like(macc)
     nacc[...] = jnp.zeros_like(nacc)
     mt[...] = jnp.zeros_like(mt)
@@ -134,8 +133,7 @@
 
     lax.fori_loop(0, 4, own_dot, 0)
 
-    for r in range(1, NY):
-        w_y(r).wait_recv()
+    done(wof.at[pl.ds(1, NY - 1), pl.ds(0, br), cols], w0r.at[0])
     for d in ZORDER:
         w_z(d).start()
     for i in range(1, NX):
@@ -190,13 +188,13 @@
             mt[p, pr : pr + 16, :] += norm_rows.astype(BF16)
 
     def a_copy(i):
-        return remote(mt.at[rem(e + i, NE)], ga.at[e], asend.at[i], arecv.at[i], ee(i))
+        return remote(mt.at[rem(e + i, NE)], ga.at[e], asend.at[0], arecv.at[0], ee(i))
 
     def b_copy(d):
         return remote(tb, gb.at[z], bsend.at[d], brecv.at[d], zz(d))
 
     def c_copy(i):
-        return remote(pc.at[rem(e + i, NE)], gc.at[e], csend.at[i], crecv.at[i], ee(i))
+        return remote(pc.at[rem(e + i, NE)], gc.at[e], csend.at[0], crecv.at[0], ee(i))
 
     for i in range(1, NE):
         a_copy(i).start()
@@ -239,8 +237,7 @@
 
     attend(0)
 
-    for i in range(1, NE):
-        a_copy(i).wait_recv()
+    done(ga.at[pl.ds(0, NE - 1)], arecv.at[0])
     plane = ga[0].astype(F32)
     for p in range(1, NE):
         plane += ga[p].astype(F32)
@@ -267,13 +264,10 @@
         c_copy(i).start()
     gc[e] = pc[e]
 
-    for i in range(1, NX):
-        for d in range(NZ):
-            w_x(i, d).wait_recv()
+    done(wof.at[pl.ds(1, NY - 1), pl.ds(0, (NX - 1) * NZ * br), cols], w2r.at[0])
     w_c().start()
 
-    for i in range(1, NE):
-        c_copy(i).wait_recv()
+    done(gc.at[pl.ds(0, NE - 1)], crecv.at[0])
     for p in range(NE):
         mem[p // per_head, (p % per_head) * pr : (p % per_head + 1) * pr, :] = gc[p, 0:pr, :]
 
@@ -281,7 +275,7 @@
 
     def m_copy(r, u):
         rows = pl.ds(u * sub, sub)
-        return remote(mixs.at[r, rows, :], mixr.at[NY - r, rows, :], msend.at[r, u], mrecv.at[r, u], yy(r))
+        return remote(mixs.at[r, rows, :], mixr.at[NY - r, rows, :], msend.at[0], mrecv.at[u], yy(r))
 
     def mix(r):
         base = rem(y + r, NY) * rc
@@ -302,16 +296,15 @@
         mix(r)
 
     w_c().wait_recv()
+    done(wof.at[0], lsem.at[2])
 
     def o_copy(r, u):
         rows = pl.ds(pl.multiple_of(y * rc + u * sub, sub), sub)
-        return remote(outs.at[r, pl.ds(u * sub, sub), :], out.at[rows, :], osend.at[r, u], orecv.at[r, u], yy(r))
-
-    keep = []
+        return remote(outs.at[r, pl.ds(u * sub, sub), :], out.at[rows, :], osend.at[0], orecv.at[0], yy(r))
+
     for u in range(NU):
         rows = slice(u * sub, (u + 1) * sub)
-        for r in range(1, NY):
-            m_copy(r, u).wait_recv()
+        done(mixr.at[pl.ds(0, NY - 1), pl.ds(0, sub), :], mrecv.at[u])
         for r in (2, 1, 3, 0):
             oc = pl.ds(pl.multiple_of(rem(y + r, NY) * fs, fs), fs)
             o = jnp.dot(mixr[0, rows, :], wof[0, :, oc], preferred_element_type=F32)
@@ -322,35 +315,20 @@
                 o_copy(r, u).start()
             else:
                 orows = pl.ds(pl.multiple_of(y * rc + u * sub, sub), sub)
-                cp = pltpu.make_async_copy(outs.at[0, pl.ds(u * sub, sub), :], out.at[orows, :], lsem.at[u])
-                cp.start()
-                keep.append(cp)
-
-    for cp in keep:
-        cp.wait()
-    for u in range(NU):
-        for r in range(1, NY):
-            o_copy(r, u).wait_recv()
-    for u in range(NU):
-        for r in range(1, NY):
-            o_copy(r, u).wait_send()
-            m_copy(r, u).wait_send()
-    for way in range(2):
-        for j in range(4):
-            t_own(j, way).wait_send()
-        for j in range(2):
-            t_far(j, way).wait_send()
-    for r in range(1, NY):
-        w_y(r).wait_send()
-    for d in range(1, NZ):
-        w_z(d).wait_send()
-    for i in range(1, NX):
-        for d in range(NZ):
-            w_x(i, d).wait_send()
+                fetch(outs.at[0, pl.ds(u * sub, sub), :], out.at[orows, :], 3)
+
+    three = pl.ds(0, NY - 1)
+    done(outs.at[0], lsem.at[3])
+    done(outs.at[three], orecv.at[0])
+    done(outs.at[three], osend.at[0])
+    done(mixs.at[three], msend.at[0])
+    done(xbuf.at[three], tsend.at[0])
+    done(wof.at[three, pl.ds(0, br), cols], w0s.at[0])
+    done(wof.at[three, pl.ds(0, (NZ - 1) * br), cols], w1s.at[0])
+    done(wof.at[three, pl.ds(0, (NX - 1) * NZ * br), cols], w2s.at[0])
     w_c().wait_send()
-    for i in range(1, NE):
-        a_copy(i).wait_send()
-        c_copy(i).wait_send()
+    done(ga.at[pl.ds(0, NE - 1)], asend.at[0])
+    done(gc.at[pl.ds(0, NE - 1)], csend.at[0])
     for d in range(1, NZ):
 
         @pl.when(z + d < NZ)
@@ -394,20 +372,20 @@
             pltpu.VMEM((NY, rc, gw), BF16),
             pltpu.VMEM((NY, rc, gw), BF16),
             pltpu.VMEM((NY, rc, fs), BF16),
-            dma((14,)),
-            dma((2, 6)), dma((2, 6)),
-            dma((NY,)), dma((NY,)),
+            dma((4,)),
+            dma((1,)), dma((2, 6)),
+            dma((1,)), dma((1,)),
+            dma((1,)), dma((NZ,)),
+            dma((1,)), dma((1,)),
+            dma((1,)), dma((1,)),
+            dma((1,)), dma((1,)),
             dma((NZ,)), dma((NZ,)),
-            dma((NX, NZ)), dma((NX, NZ)),
-            dma((1,)), dma((1,)),
-            dma((NE,)), dma((NE,)),
-            dma((NZ,)), dma((NZ,)),
-            dma((NE,)), dma((NE,)),
-            dma((NY, NU)), dma((NY, NU)),
-            dma((NY, NU)), dma((NY, NU)),
+            dma((1,)), dma((1,)),
+            dma((1,)), dma((NU,)),
+            dma((1,)), dma((1,)),
         ],
         compiler_params=pltpu.CompilerParams(
-            collective_id=0, has_side_effects=True, vmem_limit_bytes=60 * 2**20
+            collective_id=0, has_side_effects=True, vmem_limit_bytes=52 * 2**20
         ),
     )(tokens, w_query, w_key, w_value, w_out, mix_logit)
 

time: 96.5 us -> 94.1 us (0.975)
  Pallas kernels: 94.1 us -> 92.4 us
    pallas_call x1, Pallas kernels: 94.1 us -> 92.4 us  [on_device(): pl.pallas_call(kernel, out_shape=jax.ShapeDtypeStruct((seg, fs), BF16), i...]
    unnamed x1 -> x3, local copies, waits for them, and re-layouts: 2.26 us -> 1.63 us
where the time goes in v2:
time: 94.1 us
  Pallas kernels  92.4 us (98%)
  local copies, waits for them, and re-layouts  1.63 us (2%)
    pallas_call x1, Pallas kernels, on_device(): pl.pallas_call(kernel, out_shape=jax.ShapeDtypeStruct((seg, fs), BF16), i...  92.4 us

profile of v2, /device:TPU:193, one launch (start us, length us, event | category | flops | bytes accessed | tf_op | source)
XLA Modules:
  0.0 94.1 jit_solution(10793574311553444268)
XLA Ops:
  0.0 0.0 copy-start
  0.0 0.7 copy-done
  0.7 92.4 %shard_map.64 = bf16[1024,512]{1,0:T(8,128)(2,1)S(1)} custom-call(bf16[1024,512]{1,0:T(8,128)(2,1)} %tok.1, bf16[2048,512]{1,0:T(8,128)(2,1)} %wq.1, bf16[2048,512]{1,0:T(8,128)(2,1)} %wk.1, bf16[2048,512]{1,0:T(8,128)(2,1)} %wv.1, bf16[512,2048]{1,0:T(8,128)(2,1)} %wo.1, f32[2]{0:T(128)S(1)} %copy-done), custom_call_target="tpu_custom_call" | custom-call | tf_op jit(solution)/shard_map/pallas_call | solution.py:349
  93.1 1.0 %copy.8 = bf16[1024,512]{1,0:T(8,128)(2,1)} copy(bf16[1024,512]{1,0:T(8,128)(2,1)S(1)} %shard_map.64) | data formatting | bytes 2097152
Async XLA Ops:
  0.0 0.7 copy-start

commit v3 on v2

v3 whole, which is shorter than its diff:
```python
import functools

import jax
import jax.numpy as jnp
from jax import lax
from jax.experimental import pallas as pl
from jax.experimental.pallas import tpu as pltpu
from jax.sharding import Mesh
from jax.sharding import PartitionSpec as P

SEQ = ("z", "x", "c")
MESH = pl.DeviceIdType.MESH
F32, BF16 = jnp.float32, jnp.bfloat16
NZ, NX, NC, NY = 8, 4, 2, 4
NE = NX * NC
NU = 8
ZORDER = (1, 7, 2, 6, 3, 5, 4)
NT = (((1,), (1,)), ((), ()))
TN = (((0,), (0,)), ((), ()))


def feature(values):
    return jnp.where(values > 0, values + 1.0, jnp.exp(values))


def kernel(
    tok, wq, wk, wv, wo, logit, out,
    xbuf, wbuf, acc, q_s, k_s, v_s, loc, wof, macc, nacc, mt, ga, tb, gb, pc, gc, mem, mixs, outs, ls, lb,
    lsem, tsend, trecv, wys, wyr, wzs, wzr, wxs, wxr, wcs, wcr, o0s, o0r, o1s, o1r, o2s, o2r, gsend, grecv,
    asend, arecv, bsend, brecv, csend, crecv, psend, precv, dsend, drecv, fsend, frecv, osend, orecv,
):
    z, x, c, y = (lax.axis_index(a) for a in ("z", "x", "c", "y"))
    rem, div = lax.rem, lax.div
    m = div(y, 2)
    part = y + 1 - 2 * rem(y, 2)
    cross = NY - 1 - y
    g = y + c * (cross - y)
    gp = g + 1 - 2 * rem(g, 2)
    e = x * NC + m
    seg, fs = tok.shape
    heads, _, hs = q_s.shape
    rc = seg // 4
    gw = heads * hs
    pr = heads * hs // NE
    br = gw // (NZ * NX)
    wr = NY * fs // (NZ * NX)
    is_main, is_helper = c == m, c != m
    own, other = c == 0, c == 1
    at_home = c + m == 0

    def yy(r):
        return {"y": rem(y + r, NY)}

    def zz(d):
        return {"z": rem(z + d, NZ)}

    def xx(i):
        return {"x": rem(x + i, NX)}

    def ee(i):
        o = rem(e + i, NE)
        par = rem(o, NC)
        diff = par + m - 2 * par * m
        return {"x": div(o, NC), "y": y + diff * (cross - y), "c": c + diff * (1 - 2 * c)}

    sibling = {"c": 1 - c}

    def remote(src, dst, ssem, rsem, dev):
        return pltpu.make_async_remote_copy(
            src_ref=src, dst_ref=dst, send_sem=ssem, recv_sem=rsem, device_id=dev, device_id_type=MESH
        )

    def fetch(src, dst, k):
        pltpu.make_async_copy(src, dst, lsem.at[k]).start()

    def done(ref, sem):
        pltpu.make_async_copy(ref, ref, sem).wait()

    def chunk(j):
        return pl.ds(pl.multiple_of(j * rc, rc), rc)

    def block(f):
        return pl.ds(pl.multiple_of(f * fs, fs), fs)

    def group(f):
        return pl.ds(pl.multiple_of(f * gw, gw), gw)

    which = lax.broadcasted_iota(jnp.int32, ls.shape, 0)
    rows_of = jnp.zeros(ls.shape, F32)
    for h in range(heads):
        rows_of = jnp.where(which == h, logit[h], rows_of)
    ls[...] = rows_of

    weights = (wk, wv, wq)

    @pl.when(is_main)
    def _():
        fetch(tok, xbuf.at[:, block(y)], 0)

    @pl.when(own)
    def _():
        lb[...] = rows_of
        for i, w in enumerate(weights):
            fetch(w, wbuf.at[:, pl.ds(i * gw, gw)], 1)

    fetch(wo.at[:, group(g)], wof.at[0], 2)

    barrier = pltpu.get_barrier_semaphore()
    peers = [yy(r) for r in range(1, NY)] + [ee(i) for i in range(1, NE)] + [zz(d) for d in range(1, NZ)] + [sibling]
    for dev in peers:
        pl.semaphore_signal(barrier, inc=1, device_id=dev, device_id_type=MESH)
    pl.semaphore_wait(barrier, len(peers))

    def t_pair(k):
        return remote(
            tok.at[chunk(k), :], xbuf.at[chunk(k), block(y)], tsend.at[0], trecv.at[0, k], {"y": part}
        )

    def t_cross(k):
        return remote(
            tok.at[chunk(k), :], xbuf.at[chunk(k), block(y)], tsend.at[0], trecv.at[1, k], {"y": cross}
        )

    def t_on(k):
        ref = xbuf.at[chunk(k), block(cross)]
        return remote(ref, ref, tsend.at[0], trecv.at[2, k], {"y": part})

    def t_sib(k, kind, f):
        ref = xbuf.at[chunk(k), block(f)]
        return remote(ref, ref, tsend.at[0], trecv.at[kind, k], sibling)

    def t_own():
        return remote(tok, xbuf.at[:, block(y)], tsend.at[0], trecv.at[3, 0], sibling)

    def t_wait(k, kind, f):
        t_sib(k, kind, f).wait_recv()

    def w_rows(xp, zp):
        return pl.ds(pl.multiple_of((xp * NZ + zp) * wr, wr), wr)

    far_block = rem(x + 2, NX)

    def w_piece(i):
        return remote(
            weights[i].at[w_rows(x, z), :], wbuf.at[w_rows(x, z), pl.ds(i * gw, gw)], wys.at[0], wyr.at[0], {"y": cross}
        )

    def w_z(d):
        ref = wbuf.at[w_rows(x, z), :]
        return remote(ref, ref, wzs.at[0], wzr.at[d], zz(d))

    def w_x(i, d):
        ref = wbuf.at[w_rows(x, rem(z + NZ - d, NZ)), :]
        return remote(ref, ref, wxs.at[0], wxr.at[0], xx(i))

    def w_cross(i):
        return remote(
            weights[i].at[block(far_block), :], wbuf.at[block(far_block), pl.ds(i * gw, gw)],
            wcs.at[0], wcr.at[i // 2], {"y": cross, "c": 1},
        )

    def o_rows(xp, zp):
        return pl.ds(pl.multiple_of((xp * NZ + zp) * br, br), br)

    others = pl.ds(1, NY - 1)

    def o_y(r):
        yt = rem(y + r, NY)
        gt = yt + c * (NY - 1 - 2 * yt)
        return remote(
            wo.at[o_rows(x, z), group(gt)], wof.at[NY - r, o_rows(x, z), :], o0s.at[0], o0r.at[0], yy(r)
        )

    def o_z(d):
        ref = wof.at[others, o_rows(x, z), :]
        return remote(ref, ref, o1s.at[0], o1r.at[0], zz(d))

    def o_x(i):
        ref = wof.at[others, pl.ds(pl.multiple_of(x * NZ * br, NZ * br), NZ * br), :]
        return remote(ref, ref, o2s.at[0], o2r.at[0], xx(i))

    def g_copy():
        return remote(ls, lb, gsend.at[0], grecv.at[0], {"y": cross})

    @pl.when(other)
    def _():
        for i in range(3):
            w_piece(i).start()

    @pl.when(is_main)
    def _():
        for k in range(4):
            t_pair(k).start()
        t_own().start()

    @pl.when(is_helper)
    def _():
        for k in range(4):
            t_cross(k).start()

    for r in range(1, NY):
        o_y(r).start()

    @pl.when(is_helper)
    def _():
        for i in range(3):
            w_cross(i).start()

    @pl.when(other)
    def _():
        g_copy().start()

    macc[...] = jnp.zeros_like(macc)
    nacc[...] = jnp.zeros_like(nacc)
    mt[...] = jnp.zeros_like(mt)

    @pl.when(is_main)
    def _():
        done(xbuf.at[:, block(y)], lsem.at[0])

    @pl.when(is_helper)
    def _():
        t_own().wait_recv()

    @pl.when(own)
    def _():
        done(wbuf, lsem.at[1])

        def own_dot(j, carry):
            acc[chunk(j), :] = jnp.dot(
                xbuf[chunk(j), block(y)], wbuf[block(y), :], preferred_element_type=F32
            )
            return carry

        lax.fori_loop(0, 4, own_dot, 0)

    @pl.when(other)
    def _():
        done(wbuf.at[pl.ds(0, wr), :], wyr.at[0])
        for d in ZORDER:
            w_z(d).start()
        for i in (1, 3):
            w_x(i, 0).start()

    done(wof.at[others, pl.ds(0, br), :], o0r.at[0])
    for d in ZORDER:
        o_z(d).start()

    forward_at = {0: (1, 7), 1: (2, 6), 2: (3, 5), 3: (4,)}
    for k in range(4):
        t_wait(k, 0, part)
        t_wait(k, 1, cross)

        @pl.when(is_main)
        def _(k=k):
            t_on(k).start()
            t_sib(k, 1, cross).start()
            t_sib(k, 0, part).start()

        @pl.when(other)
        def _(k=k):
            for d in forward_at[k]:
                w_z(d).wait_recv()
                for i in (1, 3):
                    w_x(i, d).start()

        @pl.when(own)
        def _(k=k):
            rows = chunk(k)
            add = jnp.dot(xbuf[rows, block(part)], wbuf[block(part), :], preferred_element_type=F32)
            add += jnp.dot(xbuf[rows, block(cross)], wbuf[block(cross), :], preferred_element_type=F32)
            acc[rows, :] += add

    def finish(rows, kv):
        kv = kv.astype(BF16)
        for h in range(heads):
            key = kv[:, h * hs : (h + 1) * hs]
            val = kv[:, gw + h * hs : gw + (h + 1) * hs]
            k_s[h, rows, :] = key
            v_s[h, rows, :] = val
            fk = feature(key.astype(F32)).astype(BF16)
            macc[h] += lax.dot_general(fk, val, TN, preferred_element_type=F32)
            nacc[h] += jnp.sum(fk.astype(F32).reshape(rc // 8, 8, hs), axis=0)

    last = NY - 1 - part
    for k in range(4):
        t_wait(k, 2, last)

        @pl.when(is_main)
        def _(k=k):
            t_sib(k, 2, last).start()

        if k == 1:
            done(wof.at[others, pl.ds(0, (NZ - 1) * br), :], o1r.at[0])

            @pl.when(own)
            def _():
                for i in range(1, NX):
                    o_x(i).start()

        @pl.when(own)
        def _(k=k):
            rows = chunk(k)
            add = jnp.dot(xbuf[rows, block(last)], wbuf[block(last), 0 : 2 * gw], preferred_element_type=F32)
            finish(rows, acc[rows, 0 : 2 * gw] + add)

    @pl.when(other)
    def _():
        done(wbuf.at[pl.ds(0, 2 * NZ * wr), :], wxr.at[0])
        done(wbuf.at[pl.ds(0, fs), pl.ds(0, 2 * gw)], wcr.at[0])

        def whole(j, carry):
            rows = chunk(j)
            finish(rows, jnp.dot(xbuf[rows, :], wbuf[:, 0 : 2 * gw], preferred_element_type=F32))
            return carry

        lax.fori_loop(0, 4, whole, 0)

    per_head = hs // pr
    for h in range(heads):
        norm = jnp.sum(nacc[h], axis=0, keepdims=True)
        norm_rows = jnp.where(lax.broadcasted_iota(jnp.int32, (16, hs), 0) == h, norm, 0.0)
        for p in range(NE):
            if p // per_head == h:
                mt[p, 0:pr, :] = macc[h, (p % per_head) * pr : (p % per_head + 1) * pr, :].astype(BF16)
            mt[p, pr : pr + 16, :] += norm_rows.astype(BF16)

    def a_copy(i):
        return remote(mt.at[rem(e + i, NE)], ga.at[e], asend.at[0], arecv.at[0], ee(i))

    def b_copy(d):
        return remote(tb, gb.at[z], bsend.at[d], brecv.at[d], zz(d))

    def c_copy(i):
        return remote(pc.at[rem(e + i, NE)], gc.at[e], csend.at[0], crecv.at[0], ee(i))

    for i in range(1, NE):
        a_copy(i).start()
    ga[e] = mt[e]

    def put_q(rows, q):
        q = q.astype(BF16)
        for h in range(heads):
            q_s[h, rows, :] = q[:, h * hs : (h + 1) * hs]

    @pl.when(own)
    def _():
        def q_rows(j, carry):
            rows = chunk(j)
            add = jnp.dot(xbuf[rows, block(last)], wbuf[block(last), 2 * gw : 3 * gw], preferred_element_type=F32)
            put_q(rows, acc[rows, 2 * gw : 3 * gw] + add)
            return carry

        lax.fori_loop(0, 4, q_rows, 0)

    @pl.when(other)
    def _():
        done(wbuf.at[pl.ds(0, fs), pl.ds(2 * gw, gw)], wcr.at[1])
        g_copy().wait_recv()

        def q_rows(j, carry):
            rows = chunk(j)
            put_q(rows, jnp.dot(xbuf[rows, :], wbuf[:, 2 * gw : 3 * gw], preferred_element_type=F32))
            return carry

        lax.fori_loop(0, 4, q_rows, 0)

    shares = [jax.nn.sigmoid(lb[h : h + 1, :]) for h in range(heads)]
    scale = 1.0 / hs**0.5
    lower = lax.broadcasted_iota(jnp.int32, (rc, rc), 1) <= lax.broadcasted_iota(jnp.int32, (rc, rc), 0)

    def attend(h):
        for i in range(4):
            rows = slice(i * rc, (i + 1) * rc)
            q = q_s[h, rows, :]
            diag = lax.dot_general(q, k_s[h, rows, :], NT, preferred_element_type=F32) * scale
            diag = jnp.where(lower, diag, -1e30)
            top = jnp.max(diag, axis=1, keepdims=True)
            if i:
                before = lax.dot_general(q, k_s[h, 0 : i * rc, :], NT, preferred_element_type=F32) * scale
                top = jnp.maximum(top, jnp.max(before, axis=1, keepdims=True))
                pb = jnp.exp(before - top)
            pd = jnp.exp(diag - top)
            total = jnp.sum(pd, axis=1, keepdims=True)
            got = jnp.dot(pd.astype(BF16), v_s[h, rows, :], preferred_element_type=F32)
            if i:
                total += jnp.sum(pb, axis=1, keepdims=True)
                got += jnp.dot(pb.astype(BF16), v_s[h, 0 : i * rc, :], preferred_element_type=F32)
            loc[h, rows, :] = got / total * (1.0 - shares[h])

    attend(0)

    done(ga.at[pl.ds(0, NE - 1)], arecv.at[0])
    plane = ga[0].astype(F32)
    for p in range(1, NE):
        plane += ga[p].astype(F32)
    tb[...] = plane.astype(BF16)
    for d in range(1, NZ):

        @pl.when(z + d < NZ)
        def _(d=d):
            b_copy(d).start()

    attend(1)

    for d in range(1, NZ):

        @pl.when(z - d >= 0)
        def _(d=d):
            b_copy(d).wait_recv()

    run = lax.fori_loop(0, z, lambda k, s: s + gb[k].astype(F32), jnp.zeros(tb.shape, F32))
    for p in range(NE):
        pc[p] = run.astype(BF16)
        run += ga[p].astype(F32)
    for i in range(1, NE):
        c_copy(i).start()
    gc[e] = pc[e]

    @pl.when(other)
    def _():
        for i in range(1, NX):
            o_x(i).start()

    done(gc.at[pl.ds(0, NE - 1)], crecv.at[0])
    for p in range(NE):
        mem[p // per_head, (p % per_head) * pr : (p % per_head + 1) * pr, :] = gc[p, 0:pr, :]

    sub = seg // NU

    def m_ref(u, f):
        return mixs.at[pl.ds(u * sub, sub), group(f)]

    def m_pair(u, f):
        return remote(m_ref(u, f), m_ref(u, f), psend.at[0], precv.at[u], {"y": part})

    def m_sib(u, f):
        return remote(m_ref(u, f), m_ref(u, f), dsend.at[0], drecv.at[u], sibling)

    def m_on(u, f):
        return remote(m_ref(u, f), m_ref(u, f), fsend.at[0], frecv.at[u], sibling)

    for u in range(NU):
        rows = pl.ds(u * sub, sub)
        for h in range(heads):
            fq = feature(q_s[h, rows, :].astype(F32)).astype(BF16)
            norm = jnp.broadcast_to(gc[0, pr + h : pr + h + 1, :], (hs, hs))
            denom = lax.dot_general(fq, norm, NT, preferred_element_type=F32)
            numer = jnp.dot(fq, mem[h], preferred_element_type=F32)
            val = shares[h] * (numer / jnp.maximum(denom, 1.0)) + loc[h, rows, :]
            mixs[rows, pl.ds(pl.multiple_of(g * gw + h * hs, hs), hs)] = val.astype(BF16)
        m_pair(u, g).start()
        m_sib(u, g).start()

    done(wof.at[others, pl.ds(0, (NX - 1) * NZ * br), :], o2r.at[0])
    done(wof.at[0], lsem.at[2])

    def o_copy(u):
        rows = pl.ds(u * sub, sub)
        dev = {"y": y + c * (cross - y), "c": m}
        return remote(outs.at[rows, :], out.at[rows, :], osend.at[0], orecv.at[0], dev)

    for step in range(NU + 1):
        if step < NU:
            m_pair(step, gp).wait_recv()
            m_on(step, gp).start()
        if step:
            u = step - 1
            rows = pl.ds(u * sub, sub)
            m_sib(u, NY - 1 - g).wait_recv()
            m_on(u, NY - 1 - gp).wait_recv()
            o = jnp.dot(mixs[rows, group(y)], wof[0], preferred_element_type=F32)
            for r in range(1, NY):
                o += jnp.dot(mixs[rows, group(rem(y + r, NY))], wof[r], preferred_element_type=F32)
            outs[rows, :] = o.astype(BF16)

            @pl.when(at_home)
            def _(rows=rows):
                fetch(outs.at[rows, :], out.at[rows, :], 3)

            @pl.when(jnp.logical_not(at_home))
            def _(u=u):
                o_copy(u).start()

    @pl.when(at_home)
    def _():
        done(outs, lsem.at[3])

    @pl.when(jnp.logical_not(at_home))
    def _():
        done(outs, osend.at[0])

    @pl.when(jnp.logical_not(at_home))
    def _():
        done(outs, orecv.at[0])

    done(outs, psend.at[0])
    done(outs, dsend.at[0])
    done(outs, fsend.at[0])

    @pl.when(is_main)
    def _():
        done(wbuf, tsend.at[0])

    @pl.when(is_helper)
    def _():
        done(xbuf.at[:, pl.ds(0, fs)], tsend.at[0])
        done(wbuf.at[pl.ds(0, fs), :], wcs.at[0])

    @pl.when(other)
    def _():
        done(wbuf.at[pl.ds(0, wr), :], wys.at[0])
        done(wbuf.at[pl.ds(0, (NZ - 1) * wr), :], wzs.at[0])
        done(wbuf.at[pl.ds(0, 2 * NZ * wr), :], wxs.at[0])
        g_copy().wait_send()

    done(wof.at[others, pl.ds(0, br), :], o0s.at[0])
    done(wof.at[others, pl.ds(0, (NZ - 1) * br), :], o1s.at[0])
    done(wof.at[others, pl.ds(0, (NX - 1) * NZ * br), :], o2s.at[0])
    done(ga.at[pl.ds(0, NE - 1)], asend.at[0])
    done(gc.at[pl.ds(0, NE - 1)], csend.at[0])
    for d in range(1, NZ):

        @pl.when(z + d < NZ)
        def _(d=d):
            b_copy(d).wait_send()


def on_device(tokens, w_query, w_key, w_value, w_out, mix_logit):
    seg, fs = tokens.shape
    heads = mix_logit.shape[0]
    gw = w_query.shape[1]
    hs = gw // heads
    pr = heads * hs // NE
    hbm = pl.BlockSpec(memory_space=pl.ANY)
    dma = pltpu.SemaphoreType.DMA
    return pl.pallas_call(
        kernel,
        out_shape=jax.ShapeDtypeStruct((seg, fs), BF16),
        in_specs=[hbm] * 5 + [pl.BlockSpec(memory_space=pltpu.SMEM)],
        out_specs=hbm,
        scratch_shapes=[
            pltpu.VMEM((seg, NY * fs), BF16),
            pltpu.VMEM((NY * fs, 3 * gw), BF16),
            pltpu.VMEM((seg, 3 * gw), F32),
            pltpu.VMEM((heads, seg, hs), BF16),
            pltpu.VMEM((heads, seg, hs), BF16),
            pltpu.VMEM((heads, seg, hs), BF16),
            pltpu.VMEM((heads, seg, hs), F32),
            pltpu.VMEM((NY, gw, fs), BF16),
            pltpu.VMEM((heads, hs, hs), F32),
            pltpu.VMEM((heads, 8, hs), F32),
            pltpu.VMEM((NE, pr + 16, hs), BF16),
            pltpu.VMEM((NE, pr + 16, hs), BF16),
            pltpu.VMEM((pr + 16, hs), BF16),
            pltpu.VMEM((NZ, pr + 16, hs), BF16),
            pltpu.VMEM((NE, pr + 16, hs), BF16),
            pltpu.VMEM((NE, pr + 16, hs), BF16),
            pltpu.VMEM((heads, hs, hs), BF16),
            pltpu.VMEM((seg, NY * gw), BF16),
            pltpu.VMEM((seg, fs), BF16),
            pltpu.VMEM((8, hs), F32),
            pltpu.VMEM((8, hs), F32),
            dma((4,)),
            dma((1,)), dma((4, 4)),
            dma((1,)), dma((1,)),
            dma((1,)), dma((NZ,)),
            dma((1,)), dma((1,)),
            dma((1,)), dma((2,)),
            dma((1,)), dma((1,)),
            dma((1,)), dma((1,)),
            dma((1,)), dma((1,)),
            dma((1,)), dma((1,)),
            dma((1,)), dma((1,)),
            dma((NZ,)), dma((NZ,)),
            dma((1,)), dma((1,)),
            dma((1,)), dma((NU,)),
            dma((1,)), dma((NU,)),
            dma((1,)), dma((NU,)),
            dma((1,)), dma((1,)),
        ],
        compiler_params=pltpu.CompilerParams(
            collective_id=0, has_side_effects=True, vmem_limit_bytes=52 * 2**20
        ),
    )(tokens, w_query, w_key, w_value, w_out, mix_logit)


def solution(mesh):
    torus = Mesh(mesh.devices.reshape(NZ, NX, NC, NY), ("z", "x", "c", "y"))
    return jax.shard_map(
        on_device,
        mesh=torus,
        in_specs=(P(SEQ, "y"), P(None, "y"), P(None, "y"), P(None, "y"), P("y", None), P("y")),
        out_specs=P(SEQ, "y"),
        check_vma=False,
    )
```

time: 94.1 us -> 107 us (1.14)
  the two profiles are of different devices: /device:TPU:193 before, /device:TPU:201 now
where the time goes in v3:
time: 107 us; the launch traced here: 106 us
  Pallas kernels  105 us (98%)
  local copies, waits for them, and re-layouts  1.63 us (2%)
    pallas_call x1, Pallas kernels, on_device(): pl.pallas_call(kernel, out_shape=jax.ShapeDtypeStruct((seg, fs), BF16), i...  105 us

profile of v3, /device:TPU:201, one launch (start us, length us, event | category | flops | bytes accessed | tf_op | source)
XLA Modules:
  0.0 106.5 jit_solution(14415372550152313652)
XLA Ops:
  0.0 0.0 copy-start
  0.0 0.7 copy-done
  0.7 104.8 %shard_map.64 = bf16[1024,512]{1,0:T(8,128)(2,1)S(1)} custom-call(bf16[1024,512]{1,0:T(8,128)(2,1)} %tok.1, bf16[2048,512]{1,0:T(8,128)(2,1)} %wq.1, bf16[2048,512]{1,0:T(8,128)(2,1)} %wk.1, bf16[2048,512]{1,0:T(8,128)(2,1)} %wv.1, bf16[512,2048]{1,0:T(8,128)(2,1)} %wo.1, f32[2]{0:T(128)S(1)} %copy-done), custom_call_target="tpu_custom_call" | custom-call | tf_op jit(solution)/shard_map/pallas_call | solution.py:537
  105.5 1.0 copy.8
Async XLA Ops:
  0.0 0.7 copy-start

commit v4 on v3

--- a/solution.py
+++ b/solution.py
@@ -13,7 +13,7 @@
 F32, BF16 = jnp.float32, jnp.bfloat16
 NZ, NX, NC, NY = 8, 4, 2, 4
 NE = NX * NC
-NU = 8
+NU = 9
 ZORDER = (1, 7, 2, 6, 3, 5, 4)
 NT = (((1,), (1,)), ((), ()))
 TN = (((0,), (0,)), ((), ()))
@@ -26,7 +26,7 @@
 def kernel(
     tok, wq, wk, wv, wo, logit, out,
     xbuf, wbuf, acc, q_s, k_s, v_s, loc, wof, macc, nacc, mt, ga, tb, gb, pc, gc, mem, mixs, outs, ls, lb,
-    lsem, tsend, trecv, wys, wyr, wzs, wzr, wxs, wxr, wcs, wcr, o0s, o0r, o1s, o1r, o2s, o2r, gsend, grecv,
+    lsem, tsend, trecv, wys, wyr, wzs, wzr, wxs, wxr, wcs, wcr, o0s, o0r, o1s, o1r, o2s, o2r, o3s, o3r, gsend, grecv,
     asend, arecv, bsend, brecv, csend, crecv, psend, precv, dsend, drecv, fsend, frecv, osend, orecv,
 ):
     z, x, c, y = (lax.axis_index(a) for a in ("z", "x", "c", "y"))
@@ -85,6 +85,11 @@
     def group(f):
         return pl.ds(pl.multiple_of(f * gw, gw), gw)
 
+    barrier = pltpu.get_barrier_semaphore()
+    peers = [zz(d) for d in range(1, NZ)] + [yy(r) for r in range(1, NY)] + [ee(i) for i in range(1, NE)] + [sibling]
+    for dev in peers:
+        pl.semaphore_signal(barrier, inc=1, device_id=dev, device_id_type=MESH)
+
     which = lax.broadcasted_iota(jnp.int32, ls.shape, 0)
     rows_of = jnp.zeros(ls.shape, F32)
     for h in range(heads):
@@ -105,10 +110,6 @@
 
     fetch(wo.at[:, group(g)], wof.at[0], 2)
 
-    barrier = pltpu.get_barrier_semaphore()
-    peers = [yy(r) for r in range(1, NY)] + [ee(i) for i in range(1, NE)] + [zz(d) for d in range(1, NZ)] + [sibling]
-    for dev in peers:
-        pl.semaphore_signal(barrier, inc=1, device_id=dev, device_id_type=MESH)
     pl.semaphore_wait(barrier, len(peers))
 
     def t_pair(k):
@@ -142,16 +143,18 @@
 
     def w_piece(i):
         return remote(
-            weights[i].at[w_rows(x, z), :], wbuf.at[w_rows(x, z), pl.ds(i * gw, gw)], wys.at[0], wyr.at[0], {"y": cross}
-        )
-
-    def w_z(d):
-        ref = wbuf.at[w_rows(x, z), :]
-        return remote(ref, ref, wzs.at[0], wzr.at[d], zz(d))
-
-    def w_x(i, d):
-        ref = wbuf.at[w_rows(x, rem(z + NZ - d, NZ)), :]
-        return remote(ref, ref, wxs.at[0], wxr.at[0], xx(i))
+            weights[i].at[w_rows(x, z), :], wbuf.at[w_rows(x, z), pl.ds(i * gw, gw)], wys.at[0], wyr.at[i // 2], {"y": cross}
+        )
+
+    w_cols = (pl.ds(0, 2 * gw), pl.ds(2 * gw, gw))
+
+    def w_z(kind, d):
+        ref = wbuf.at[w_rows(x, z), w_cols[kind]]
+        return remote(ref, ref, wzs.at[0], wzr.at[kind, d], zz(d))
+
+    def w_x(kind, i, d):
+        ref = wbuf.at[w_rows(x, rem(z + NZ - d, NZ)), w_cols[kind]]
+        return remote(ref, ref, wxs.at[0], wxr.at[kind], xx(i))
 
     def w_cross(i):
         return remote(
@@ -162,22 +165,28 @@
     def o_rows(xp, zp):
         return pl.ds(pl.multiple_of((xp * NZ + zp) * br, br), br)
 
-    others = pl.ds(1, NY - 1)
-
-    def o_y(r):
-        yt = rem(y + r, NY)
-        gt = yt + c * (NY - 1 - 2 * yt)
+    def o_y():
         return remote(
-            wo.at[o_rows(x, z), group(gt)], wof.at[NY - r, o_rows(x, z), :], o0s.at[0], o0r.at[0], yy(r)
+            wo.at[o_rows(x, z), group(NY - 1 - gp)], wof.at[2, o_rows(x, z), :], o0s.at[0], o0r.at[0], yy(2)
         )
 
     def o_z(d):
-        ref = wof.at[others, o_rows(x, z), :]
+        ref = wof.at[2, o_rows(x, z), :]
         return remote(ref, ref, o1s.at[0], o1r.at[0], zz(d))
 
     def o_x(i):
-        ref = wof.at[others, pl.ds(pl.multiple_of(x * NZ * br, NZ * br), NZ * br), :]
+        ref = wof.at[2, pl.ds(pl.multiple_of(x * NZ * br, NZ * br), NZ * br), :]
         return remote(ref, ref, o2s.at[0], o2r.at[0], xx(i))
+
+    def o_pair():
+        return remote(
+            wo.at[:, group(gp)], wof.at[3 - 2 * rem(y, 2)], o3s.at[0], o3r.at[0], {"y": part}
+        )
+
+    def o_cross():
+        return remote(
+            wo.at[:, group(NY - 1 - g)], wof.at[1 + 2 * rem(y, 2)], o3s.at[0], o3r.at[1], {"y": cross}
+        )
 
     def g_copy():
         return remote(ls, lb, gsend.at[0], grecv.at[0], {"y": cross})
@@ -186,6 +195,8 @@
     def _():
         for i in range(3):
             w_piece(i).start()
+
+    o_y().start()
 
     @pl.when(is_main)
     def _():
@@ -197,12 +208,6 @@
     def _():
         for k in range(4):
             t_cross(k).start()
-
-    for r in range(1, NY):
-        o_y(r).start()
-
-    @pl.when(is_helper)
-    def _():
         for i in range(3):
             w_cross(i).start()
 
@@ -236,15 +241,11 @@
 
     @pl.when(other)
     def _():
-        done(wbuf.at[pl.ds(0, wr), :], wyr.at[0])
+        done(wbuf.at[pl.ds(0, wr), pl.ds(0, 2 * gw)], wyr.at[0])
         for d in ZORDER:
-            w_z(d).start()
+            w_z(0, d).start()
         for i in (1, 3):
-            w_x(i, 0).start()
-
-    done(wof.at[others, pl.ds(0, br), :], o0r.at[0])
-    for d in ZORDER:
-        o_z(d).start()
+            w_x(0, i, 0).start()
 
     forward_at = {0: (1, 7), 1: (2, 6), 2: (3, 5), 3: (4,)}
     for k in range(4):
@@ -260,9 +261,9 @@
         @pl.when(other)
         def _(k=k):
             for d in forward_at[k]:
-                w_z(d).wait_recv()
+                w_z(0, d).wait_recv()
                 for i in (1, 3):
-                    w_x(i, d).start()
+                    w_x(0, i, d).start()
 
         @pl.when(own)
         def _(k=k):
@@ -282,6 +283,18 @@
             macc[h] += lax.dot_general(fk, val, TN, preferred_element_type=F32)
             nacc[h] += jnp.sum(fk.astype(F32).reshape(rc // 8, 8, hs), axis=0)
 
+    @pl.when(other)
+    def _():
+        done(wbuf.at[pl.ds(0, wr), pl.ds(0, gw)], wyr.at[1])
+        for d in ZORDER:
+            w_z(1, d).start()
+        for i in (1, 3):
+            w_x(1, i, 0).start()
+
+    done(wof.at[2, pl.ds(0, br), :], o0r.at[0])
+    for d in ZORDER:
+        o_z(d).start()
+
     last = NY - 1 - part
     for k in range(4):
         t_wait(k, 2, last)
@@ -290,13 +303,12 @@
         def _(k=k):
             t_sib(k, 2, last).start()
 
-        if k == 1:
-            done(wof.at[others, pl.ds(0, (NZ - 1) * br), :], o1r.at[0])
-
-            @pl.when(own)
-            def _():
-                for i in range(1, NX):
-                    o_x(i).start()
+        @pl.when(other)
+        def _(k=k):
+            rows = chunk(k)
+            acc[rows, 0 : 2 * gw] = jnp.dot(
+                xbuf[rows, block(x)], wbuf[block(x), 0 : 2 * gw], preferred_element_type=F32
+            )
 
         @pl.when(own)
         def _(k=k):
@@ -306,12 +318,20 @@
 
     @pl.when(other)
     def _():
-        done(wbuf.at[pl.ds(0, 2 * NZ * wr), :], wxr.at[0])
+        for d in ZORDER:
+            w_z(1, d).wait_recv()
+            for i in (1, 3):
+                w_x(1, i, d).start()
+        done(wbuf.at[pl.ds(0, 2 * NZ * wr), pl.ds(0, 2 * gw)], wxr.at[0])
         done(wbuf.at[pl.ds(0, fs), pl.ds(0, 2 * gw)], wcr.at[0])
 
         def whole(j, carry):
             rows = chunk(j)
-            finish(rows, jnp.dot(xbuf[rows, :], wbuf[:, 0 : 2 * gw], preferred_element_type=F32))
+            kv = acc[rows, 0 : 2 * gw]
+            for i in range(1, NX):
+                f = block(rem(x + i, NX))
+                kv += jnp.dot(xbuf[rows, f], wbuf[f, 0 : 2 * gw], preferred_element_type=F32)
+            finish(rows, kv)
             return carry
 
         lax.fori_loop(0, 4, whole, 0)
@@ -337,6 +357,22 @@
     for i in range(1, NE):
         a_copy(i).start()
     ga[e] = mt[e]
+    o_pair().start()
+    o_cross().start()
+    done(wof.at[2, pl.ds(0, (NZ - 1) * br), :], o1r.at[0])
+    for i in range(1, NX):
+        o_x(i).start()
+
+    done(ga.at[pl.ds(0, NE - 1)], arecv.at[0])
+    plane = ga[0].astype(F32)
+    for p in range(1, NE):
+        plane += ga[p].astype(F32)
+    tb[...] = plane.astype(BF16)
+    for d in range(1, NZ):
+
+        @pl.when(z + d < NZ)
+        def _(d=d):
+            b_copy(d).start()
 
     def put_q(rows, q):
         q = q.astype(BF16)
@@ -355,7 +391,8 @@
 
     @pl.when(other)
     def _():
-        done(wbuf.at[pl.ds(0, fs), pl.ds(2 * gw, gw)], wcr.at[1])
+        done(wbuf.at[pl.ds(0, fs), pl.ds(0, gw)], wcr.at[1])
+        done(wbuf.at[pl.ds(0, 2 * NZ * wr), pl.ds(0, gw)], wxr.at[1])
         g_copy().wait_recv()
 
         def q_rows(j, carry):
@@ -390,17 +427,6 @@
 
     attend(0)
 
-    done(ga.at[pl.ds(0, NE - 1)], arecv.at[0])
-    plane = ga[0].astype(F32)
-    for p in range(1, NE):
-        plane += ga[p].astype(F32)
-    tb[...] = plane.astype(BF16)
-    for d in range(1, NZ):
-
-        @pl.when(z + d < NZ)
-        def _(d=d):
-            b_copy(d).start()
-
     attend(1)
 
     for d in range(1, NZ):
@@ -417,19 +443,15 @@
         c_copy(i).start()
     gc[e] = pc[e]
 
-    @pl.when(other)
-    def _():
-        for i in range(1, NX):
-            o_x(i).start()
-
     done(gc.at[pl.ds(0, NE - 1)], crecv.at[0])
     for p in range(NE):
         mem[p // per_head, (p % per_head) * pr : (p % per_head + 1) * pr, :] = gc[p, 0:pr, :]
 
-    sub = seg // NU
+    sizes = [seg // 8] * 7 + [seg // 16] * 2
+    spans = [(sum(sizes[:u]), size) for u, size in enumerate(sizes)]
 
     def m_ref(u, f):
-        return mixs.at[pl.ds(u * sub, sub), group(f)]
+        return mixs.at[pl.ds(*spans[u]), group(f)]
 
     def m_pair(u, f):
         return remote(m_ref(u, f), m_ref(u, f), psend.at[0], precv.at[u], {"y": part})
@@ -441,7 +463,7 @@
         return remote(m_ref(u, f), m_ref(u, f), fsend.at[0], frecv.at[u], sibling)
 
     for u in range(NU):
-        rows = pl.ds(u * sub, sub)
+        rows = pl.ds(*spans[u])
         for h in range(heads):
             fq = feature(q_s[h, rows, :].astype(F32)).astype(BF16)
             norm = jnp.broadcast_to(gc[0, pr + h : pr + h + 1, :], (hs, hs))
@@ -452,11 +474,8 @@
         m_pair(u, g).start()
         m_sib(u, g).start()
 
-    done(wof.at[others, pl.ds(0, (NX - 1) * NZ * br), :], o2r.at[0])
-    done(wof.at[0], lsem.at[2])
-
     def o_copy(u):
-        rows = pl.ds(u * sub, sub)
+        rows = pl.ds(*spans[u])
         dev = {"y": y + c * (cross - y), "c": m}
         return remote(outs.at[rows, :], out.at[rows, :], osend.at[0], orecv.at[0], dev)
 
@@ -466,7 +485,12 @@
             m_on(step, gp).start()
         if step:
             u = step - 1
-            rows = pl.ds(u * sub, sub)
+            if u == 0:
+                done(wof.at[2, pl.ds(0, (NX - 1) * NZ * br), :], o2r.at[0])
+                done(wof.at[0], o3r.at[0])
+                done(wof.at[0], o3r.at[1])
+                done(wof.at[0], lsem.at[2])
+            rows = pl.ds(*spans[u])
             m_sib(u, NY - 1 - g).wait_recv()
             m_on(u, NY - 1 - gp).wait_recv()
             o = jnp.dot(mixs[rows, group(y)], wof[0], preferred_element_type=F32)
@@ -514,9 +538,10 @@
         done(wbuf.at[pl.ds(0, 2 * NZ * wr), :], wxs.at[0])
         g_copy().wait_send()
 
-    done(wof.at[others, pl.ds(0, br), :], o0s.at[0])
-    done(wof.at[others, pl.ds(0, (NZ - 1) * br), :], o1s.at[0])
-    done(wof.at[others, pl.ds(0, (NX - 1) * NZ * br), :], o2s.at[0])
+    done(wof.at[2, pl.ds(0, br), :], o0s.at[0])
+    done(wof.at[2, pl.ds(0, (NZ - 1) * br), :], o1s.at[0])
+    done(wof.at[2, pl.ds(0, (NX - 1) * NZ * br), :], o2s.at[0])
+    done(wof.at[pl.ds(0, 2)], o3s.at[0])
     done(ga.at[pl.ds(0, NE - 1)], asend.at[0])
     done(gc.at[pl.ds(0, NE - 1)], csend.at[0])
     for d in range(1, NZ):
@@ -563,13 +588,14 @@
             pltpu.VMEM((8, hs), F32),
             dma((4,)),
             dma((1,)), dma((4, 4)),
-            dma((1,)), dma((1,)),
-            dma((1,)), dma((NZ,)),
-            dma((1,)), dma((1,)),
+            dma((1,)), dma((2,)),
+            dma((1,)), dma((2, NZ)),
+            dma((1,)), dma((2,)),
             dma((1,)), dma((2,)),
             dma((1,)), dma((1,)),
             dma((1,)), dma((1,)),
             dma((1,)), dma((1,)),
+            dma((1,)), dma((2,)),
             dma((1,)), dma((1,)),
             dma((1,)), dma((1,)),
             dma((NZ,)), dma((NZ,)),

time: 107 us -> 94.3 us (0.88)
  the two profiles are of different devices: /device:TPU:201 before, /device:TPU:1 now
where the time goes in v4:
time: 94.3 us; the launch traced here: 94.2 us
  Pallas kernels  92.6 us (98%)
  local copies, waits for them, and re-layouts  1.63 us (2%)
    pallas_call x1, Pallas kernels, on_device(): pl.pallas_call(kernel, out_shape=jax.ShapeDtypeStruct((seg, fs), BF16), i...  92.6 us

profile of v4, /device:TPU:1, one launch (start us, length us, event | category | flops | bytes accessed | tf_op | source)
XLA Modules:
  0.0 94.2 jit_solution(18172830524233180654)
XLA Ops:
  0.0 0.0 copy-start
  0.0 0.7 copy-done
  0.7 92.6 %shard_map.64 = bf16[1024,512]{1,0:T(8,128)(2,1)S(1)} custom-call(bf16[1024,512]{1,0:T(8,128)(2,1)} %tok.1, bf16[2048,512]{1,0:T(8,128)(2,1)} %wq.1, bf16[2048,512]{1,0:T(8,128)(2,1)} %wk.1, bf16[2048,512]{1,0:T(8,128)(2,1)} %wv.1, bf16[512,2048]{1,0:T(8,128)(2,1)} %wo.1, f32[2]{0:T(128)S(1)} %copy-done), custom_call_target="tpu_custom_call" | custom-call | tf_op jit(solution)/shard_map/pallas_call | solution.py:562
  93.2 1.0 %copy.8 = bf16[1024,512]{1,0:T(8,128)(2,1)} copy(bf16[1024,512]{1,0:T(8,128)(2,1)S(1)} %shard_map.64) | data formatting | bytes 2097152
Async XLA Ops:
  0.0 0.7 copy-start

commit v5 on v4

v5 whole, which is shorter than its diff:
```python
import functools

import jax
import jax.numpy as jnp
from jax import lax
from jax.experimental import pallas as pl
from jax.experimental.pallas import tpu as pltpu
from jax.sharding import Mesh
from jax.sharding import PartitionSpec as P

SEQ = ("z", "x", "c")
MESH = pl.DeviceIdType.MESH
F32, BF16 = jnp.float32, jnp.bfloat16
NZ, NX, NC, NY = 8, 4, 2, 4
NE = NX * NC
NU = 9
ZORDER = (1, 7, 2, 6, 3, 5, 4)
NT = (((1,), (1,)), ((), ()))
TN = (((0,), (0,)), ((), ()))


def feature(values):
    return jnp.where(values > 0, values + 1.0, jnp.exp(values))


def kernel(
    tok, wq, wk, wv, wo, logit, out,
    xbuf, wbuf, acc, q_s, k_s, v_s, loc, wof, macc, nacc, mt, ga, tb, gb, pc, gc, mem, nrm, mixs, outs, ls, lb,
    lsem, tsend, trecv, wys, wyr, wzs, wzr, wqr, wxs, wxr, wcs, wcr, o0s, o0r, o1s, o1r, o2s, o2r, o3s, o3r, gsend, grecv,
    asend, arecv, bsend, brecv, csend, crecv, psend, precv, dsend, drecv, fsend, osend, orecv,
):
    z, x, c, y = (lax.axis_index(a) for a in ("z", "x", "c", "y"))
    rem, div = lax.rem, lax.div
    m = div(y, 2)
    part = y + 1 - 2 * rem(y, 2)
    cross = NY - 1 - y
    g = y + c * (cross - y)
    gp = g + 1 - 2 * rem(g, 2)
    e = x * NC + m
    seg, fs = tok.shape
    heads, _, hs = q_s.shape
    rc = seg // 4
    gw = heads * hs
    pr = heads * hs // NE
    br = gw // (NZ * NX)
    wr = NY * fs // (NZ * NX)
    is_source, not_source = c == m, c != m
    is_main = c == 1
    at_home = c + m == 0

    def yy(r):
        return {"y": rem(y + r, NY)}

    def zz(d):
        return {"z": rem(z + d, NZ)}

    def xx(i):
        return {"x": rem(x + i, NX)}

    def ee(i):
        o = rem(e + i, NE)
        par = rem(o, NC)
        diff = par + m - 2 * par * m
        return {"x": div(o, NC), "y": y + diff * (cross - y)}

    sibling = {"c": 1 - c}

    def remote(src, dst, ssem, rsem, dev):
        return pltpu.make_async_remote_copy(
            src_ref=src, dst_ref=dst, send_sem=ssem, recv_sem=rsem, device_id=dev, device_id_type=MESH
        )

    def fetch(src, dst, k):
        pltpu.make_async_copy(src, dst, lsem.at[k]).start()

    def done(ref, sem):
        pltpu.make_async_copy(ref, ref, sem).wait()

    def chunk(j):
        return pl.ds(pl.multiple_of(j * rc, rc), rc)

    def block(f):
        return pl.ds(pl.multiple_of(f * fs, fs), fs)

    def group(f):
        return pl.ds(pl.multiple_of(f * gw, gw), gw)

    barrier = pltpu.get_barrier_semaphore()
    peers = [zz(d) for d in range(1, NZ)] + [yy(r) for r in range(1, NY)] + [xx(i) for i in range(1, NX)]
    peers += [{"x": rem(x + i, NX), "y": cross} for i in range(1, NX)] + [sibling, {"y": cross, "c": 1 - c}, {"y": part, "c": 1 - c}]
    for dev in peers:
        pl.semaphore_signal(barrier, inc=1, device_id=dev, device_id_type=MESH)

    ls[...] = jnp.full(ls.shape, logit[c], F32)

    weights = (wk, wv, wq)
    nh = 3 * hs
    ok, oq = slice(0, 2 * hs), slice(2 * hs, nh)
    ck, cq = slice(nh, nh + 2 * hs), slice(nh + 2 * hs, 2 * nh)

    def head(ct):
        return pl.ds(pl.multiple_of(ct * hs, hs), hs)

    @pl.when(is_source)
    def _():
        fetch(tok, xbuf.at[:, block(y)], 0)

    for i, w in enumerate(weights):
        fetch(w.at[:, head(c)], wbuf.at[:, pl.ds(i * hs, hs)], 1)

    fetch(wo.at[:, group(g)], wof.at[0], 2)

    pl.semaphore_wait(barrier, len(peers))

    def t_pair(k):
        return remote(
            tok.at[chunk(k), :], xbuf.at[chunk(k), block(y)], tsend.at[0], trecv.at[0, k], {"y": part, "c": 1}
        )

    def t_cross(k):
        return remote(
            tok.at[chunk(k), :], xbuf.at[chunk(k), block(y)], tsend.at[0], trecv.at[0, k], {"y": cross, "c": 1}
        )

    def t_on(k):
        ref = xbuf.at[chunk(k), block(cross)]
        return remote(ref, ref, tsend.at[1], trecv.at[1, k], {"y": part})

    def t_sib(k, kind, f):
        ref = xbuf.at[chunk(k), block(f)]
        return remote(ref, ref, tsend.at[1], trecv.at[kind, k], sibling)

    def t_own():
        return remote(tok, xbuf.at[:, block(y)], tsend.at[0], trecv.at[2, 0], sibling)

    def t_wait(k, kind, f):
        t_sib(k, kind, f).wait_recv()

    def w_rows(xp, zp):
        return pl.ds(pl.multiple_of((xp * NZ + zp) * wr, wr), wr)

    far_block = rem(x + 2, NX)
    w_cols = (pl.ds(nh, 2 * hs), pl.ds(nh + 2 * hs, hs), pl.ds(nh + hs, hs))

    def w_piece(i):
        return remote(
            weights[i].at[w_rows(x, z), head(c)], wbuf.at[w_rows(x, z), pl.ds(nh + i * hs, hs)],
            wys.at[0], wyr.at[i // 2], {"y": cross},
        )

    def w_z(kind, d):
        ref = wbuf.at[w_rows(x, z), w_cols[kind]]
        return remote(ref, ref, wzs.at[0], wqr.at[0] if kind else wzr.at[d], zz(d))

    def w_x(kind, i, d):
        ref = wbuf.at[w_rows(x, rem(z + NZ - d, NZ)), w_cols[kind]]
        return remote(ref, ref, wxs.at[kind], wxr.at[kind], xx(i))

    def w_xs(d):
        w_x(0, 1, d).start()
        w_x(0, 3, d).start()
        w_x(2, 2, d).start()

    def w_cross(i, ct):
        return remote(
            weights[i].at[block(far_block), head(ct)], wbuf.at[block(far_block), pl.ds(nh + i * hs, hs)],
            wcs.at[0], wcr.at[i // 2], {"y": cross, "c": ct},
        )

    def o_rows(xp, zp):
        return pl.ds(pl.multiple_of((xp * NZ + zp) * br, br), br)

    def o_y():
        return remote(
            wo.at[o_rows(x, z), group(NY - 1 - gp)], wof.at[2, o_rows(x, z), :], o0s.at[0], o0r.at[0], yy(2)
        )

    def o_z(d):
        ref = wof.at[2, o_rows(x, z), :]
        return remote(ref, ref, o1s.at[0], o1r.at[0], zz(d))

    def o_x(i):
        ref = wof.at[2, pl.ds(pl.multiple_of(x * NZ * br, NZ * br), NZ * br), :]
        return remote(ref, ref, o2s.at[0], o2r.at[0], xx(i))

    def o_pair():
        return remote(
            wo.at[:, group(gp)], wof.at[3 - 2 * rem(y, 2)], o3s.at[0], o3r.at[0], {"y": part}
        )

    def o_cross():
        return remote(
            wo.at[:, group(NY - 1 - g)], wof.at[1 + 2 * rem(y, 2)], o3s.at[0], o3r.at[1], {"y": cross}
        )

    def g_copy():
        return remote(ls, lb, gsend.at[0], grecv.at[0], {"y": cross})

    for i in range(2):
        w_piece(i).start()
    o_y().start()

    @pl.when(is_source)
    def _():
        for k in range(4):
            t_pair(k).start()
        t_own().start()

    @pl.when(not_source)
    def _():
        for k in range(4):
            t_cross(k).start()

    w_piece(2).start()
    g_copy().start()

    @pl.when(not_source)
    def _():
        for i in (0, 2):
            for ct in (1, 0):
                w_cross(i, ct).start()
        o_cross().start()

    macc[...] = jnp.zeros_like(macc)
    nacc[...] = jnp.zeros_like(nacc)

    @pl.when(is_source)
    def _():
        done(xbuf.at[:, block(y)], lsem.at[0])

    @pl.when(not_source)
    def _():
        t_own().wait_recv()

    done(wbuf.at[:, pl.ds(0, nh)], lsem.at[1])

    def own_dot(j, carry):
        acc[chunk(j), 0:nh] = jnp.dot(
            xbuf[chunk(j), block(y)], wbuf[block(y), 0:nh], preferred_element_type=F32
        )
        return carry

    lax.fori_loop(0, 2, own_dot, 0)
    done(wbuf.at[pl.ds(0, wr), pl.ds(0, 2 * hs)], wyr.at[0])
    for d in ZORDER:
        w_z(0, d).start()
    w_xs(0)
    lax.fori_loop(2, 4, own_dot, 0)

    forward_at = {0: (1, 7), 1: (2, 6), 2: (3, 5), 3: (4,)}
    for k in range(4):
        done(xbuf.at[chunk(k), pl.ds(0, 2 * fs)], trecv.at[0, k])

        @pl.when(is_main)
        def _(k=k):
            t_on(k).start()
            t_sib(k, 0, cross).start()
            t_sib(k, 0, part).start()

        for d in forward_at[k]:
            w_z(0, d).wait_recv()
            w_xs(d)
        rows = chunk(k)
        add = jnp.dot(xbuf[rows, block(part)], wbuf[block(part), 0:nh], preferred_element_type=F32)
        add += jnp.dot(xbuf[rows, block(cross)], wbuf[block(cross), 0:nh], preferred_element_type=F32)
        acc[rows, 0:nh] += add

    def finish(h, rows, kv):
        kv = kv.astype(BF16)
        key, val = kv[:, :hs], kv[:, hs:]
        k_s[h, rows, :] = key
        v_s[h, rows, :] = val
        fk = feature(key.astype(F32)).astype(BF16)
        macc[h] += lax.dot_general(fk, val, TN, preferred_element_type=F32)
        nacc[h] += jnp.sum(fk.astype(F32).reshape(rc // 8, 8, hs), axis=0)

    def cross_rows(j):
        rows = chunk(j)
        kv = acc[rows, ck]
        for i in range(1, NX):
            f = block(rem(x + i, NX))
            kv += jnp.dot(xbuf[rows, f], wbuf[f, ck], preferred_element_type=F32)
        finish(1, rows, kv)

    done(wbuf.at[pl.ds(0, wr), pl.ds(0, hs)], wyr.at[1])
    for d in ZORDER:
        w_z(1, d).start()
    w_x(1, 1, 0).start()
    w_x(1, 3, 0).start()

    done(wof.at[2, pl.ds(0, br), :], o0r.at[0])
    for d in ZORDER:
        o_z(d).start()

    def q_forward():
        done(wbuf.at[pl.ds(0, wr * (NZ - 1)), pl.ds(0, hs)], wqr.at[0])
        for d in ZORDER:
            w_x(1, 1, d).start()
            w_x(1, 3, d).start()

    last = NY - 1 - part
    for k in range(4):
        if k == 3:
            done(wbuf.at[pl.ds(0, 2 * NZ * wr), pl.ds(0, 2 * hs)], wxr.at[0])
            done(wbuf.at[pl.ds(0, fs), pl.ds(0, hs)], wxr.at[2])
            done(wbuf.at[pl.ds(0, fs), pl.ds(0, hs)], wcr.at[0])

            for j in range(3):
                cross_rows(j)
            pl.when(c == 1)(q_forward)

        t_wait(k, 1, last)

        @pl.when(is_main)
        def _(k=k):
            t_sib(k, 1, last).start()

        rows = chunk(k)
        acc[rows, ck] = jnp.dot(xbuf[rows, block(x)], wbuf[block(x), ck], preferred_element_type=F32)
        add = jnp.dot(xbuf[rows, block(last)], wbuf[block(last), ok], preferred_element_type=F32)
        finish(0, rows, acc[rows, ok] + add)

    cross_rows(3)

    per_head, hw = hs // pr, hs // 2
    norms = []
    for h in range(heads):
        slot = m if h == 0 else 1 - m
        norm = jnp.sum(nacc[h], axis=0, keepdims=True)
        which = lax.broadcasted_iota(jnp.int32, (16, hw), 0)
        norms += [jnp.where(which == 2 * slot + i, norm[:, i * hw : (i + 1) * hw], 0.0) for i in range(2)]
        for p in range(per_head):
            rows = slice(p * pr, (p + 1) * pr)
            for i in range(2):
                mt[slot * per_head + p, i * pr : (i + 1) * pr, :] = macc[h, rows, i * hw : (i + 1) * hw].astype(BF16)
    for p in range(NE):
        mt[p, 2 * pr :, :] = sum(norms).astype(BF16)

    def a_copy(i):
        return remote(mt.at[rem(e + i, NE)], ga.at[e], asend.at[0], arecv.at[0], ee(i))

    def b_copy(d):
        return remote(tb, gb.at[z], bsend.at[0], brecv.at[0], zz(d))

    def c_copy(i):
        return remote(pc.at[rem(e + i, NE)], gc.at[e], csend.at[0], crecv.at[0], ee(i))

    for i in range(1, NE):
        a_copy(i).start()
    ga[e] = mt[e]
    o_pair().start()
    pl.when(c == 0)(q_forward)

    scale = 1.0 / hs**0.5
    lower = lax.broadcasted_iota(jnp.int32, (rc, rc), 1) <= lax.broadcasted_iota(jnp.int32, (rc, rc), 0)

    def attend(h):
        for i in range(4):
            rows = slice(i * rc, (i + 1) * rc)
            q = q_s[h, rows, :]
            diag = lax.dot_general(q, k_s[h, rows, :], NT, preferred_element_type=F32) * scale
            diag = jnp.where(lower, diag, -1e30)
            top = jnp.max(diag, axis=1, keepdims=True)
            if i:
                before = lax.dot_general(q, k_s[h, 0 : i * rc, :], NT, preferred_element_type=F32) * scale
                top = jnp.maximum(top, jnp.max(before, axis=1, keepdims=True))
                pb = jnp.exp(before - top)
            pd = jnp.exp(diag - top)
            total = jnp.sum(pd, axis=1, keepdims=True)
            got = jnp.dot(pd.astype(BF16), v_s[h, rows, :], preferred_element_type=F32)
            if i:
                total += jnp.sum(pb, axis=1, keepdims=True)
                got += jnp.dot(pb.astype(BF16), v_s[h, 0 : i * rc, :], preferred_element_type=F32)
            loc[h, rows, :] = got / total * (1.0 - shares[h])

    def own_q(j, carry):
        rows = chunk(j)
        add = jnp.dot(xbuf[rows, block(last)], wbuf[block(last), oq], preferred_element_type=F32)
        q_s[0, rows, :] = (acc[rows, oq] + add).astype(BF16)
        return carry

    lax.fori_loop(0, 4, own_q, 0)
    shares = [jax.nn.sigmoid(ls[0:1, :])]
    attend(0)

    done(ga.at[pl.ds(0, NE - 1)], arecv.at[0])
    plane = ga[0].astype(F32)
    for p in range(1, NE):
        plane += ga[p].astype(F32)
    tb[...] = plane.astype(BF16)
    for d in (4, 3, 5, 2, 6, 1, 7):

        @pl.when(z + d < NZ)
        def _(d=d):
            b_copy(d).start()

    def bulk():
        @pl.when(is_source)
        def _():
            o_cross().start()

        for i in range(1, NX):
            o_x(i).start()

    done(wof.at[2, pl.ds(0, (NZ - 1) * br), :], o1r.at[0])
    pl.when(c == 0)(bulk)

    done(wbuf.at[pl.ds(0, fs), pl.ds(0, hs)], wcr.at[1])
    done(wbuf.at[pl.ds(0, 2 * NZ * wr), pl.ds(0, hs)], wxr.at[1])
    g_copy().wait_recv()

    def cross_q(j, carry):
        rows = chunk(j)
        q_s[1, rows, :] = jnp.dot(xbuf[rows, :], wbuf[:, cq], preferred_element_type=F32).astype(BF16)
        return carry

    lax.fori_loop(0, 4, cross_q, 0)
    shares.append(jax.nn.sigmoid(lb[0:1, :]))

    attend(1)

    for n in range(1, NZ):

        @pl.when(z == n)
        def _(n=n):
            done(gb.at[pl.ds(0, n)], brecv.at[0])

    run = lax.fori_loop(0, z, lambda k, s: s + gb[k].astype(F32), jnp.zeros(tb.shape, F32))
    for p in range(NE):
        pc[p] = run.astype(BF16)
        run += ga[p].astype(F32)
    for i in range(1, NE):
        c_copy(i).start()
    gc[e] = pc[e]
    pl.when(c == 1)(bulk)

    done(gc.at[pl.ds(0, NE - 1)], crecv.at[0])
    for h in range(heads):
        slot = m if h == 0 else 1 - m
        for p in range(per_head):
            for i in range(2):
                mem[h, p * pr : (p + 1) * pr, i * hw : (i + 1) * hw] = gc[slot * per_head + p, i * pr : (i + 1) * pr, :]
        for i in range(2):
            row = 2 * pr + i
            norm = jnp.where(slot == 0, gc[0, row : row + 1, :].astype(F32), gc[0, row + 2 : row + 3, :].astype(F32))
            nrm[h, :, i * hw : (i + 1) * hw] = jnp.broadcast_to(norm, (hs, hw)).astype(BF16)

    sizes = [seg // 8] * 7 + [seg // 16] * 2
    spans = [(sum(sizes[:u]), size) for u, size in enumerate(sizes)]

    pidx = div(y * cross, 2)

    def m_ref(u, cc, pp):
        return mixs.at[pl.ds(*spans[u]), pl.ds(pl.multiple_of(cc * 4 * hs + pp * 2 * hs, hs), 2 * hs)]

    def m_pair(u, pp):
        return remote(m_ref(u, c, pp), m_ref(u, c, pp), psend.at[0], precv.at[u], {"y": part})

    def m_sib(u, pp, fin):
        return remote(m_ref(u, c, pp), m_ref(u, c, pp), fin.at[0], drecv.at[u], sibling)

    for u in range(NU):
        rows = pl.ds(*spans[u])
        for h in range(heads):
            fq = feature(q_s[h, rows, :].astype(F32)).astype(BF16)
            denom = lax.dot_general(fq, nrm[h], NT, preferred_element_type=F32)
            numer = jnp.dot(fq, mem[h], preferred_element_type=F32)
            val = shares[h] * (numer / jnp.maximum(denom, 1.0)) + loc[h, rows, :]
            at = c * 4 * hs + pidx * 2 * hs + (m if h == 0 else 1 - m) * hs
            mixs[rows, pl.ds(pl.multiple_of(at, hs), hs)] = val.astype(BF16)
        m_pair(u, pidx).start()
        m_sib(u, pidx, dsend).start()

    def o_copy(u):
        rows = pl.ds(*spans[u])
        dev = {"y": y + c * (cross - y), "c": m}
        return remote(outs.at[rows, :], out.at[rows, :], osend.at[0], orecv.at[0], dev)

    for step in range(NU + 1):
        if step < NU:
            m_pair(step, 1 - pidx).wait_recv()
            m_sib(step, 1 - pidx, fsend).start()
        if step:
            u = step - 1
            if u == 0:
                done(wof.at[2, pl.ds(0, (NX - 1) * NZ * br), :], o2r.at[0])
                done(wof.at[0], o3r.at[0])
                done(wof.at[0], o3r.at[1])
                done(wof.at[0], lsem.at[2])
            rows = pl.ds(*spans[u])
            done(mixs.at[rows, pl.ds(0, 2 * gw)], drecv.at[u])
            o = jnp.zeros((spans[u][1], fs), F32)
            for cc in range(NC):
                for pos, grp in enumerate((0, 3, 1, 2)):
                    at = cc * 4 * hs + pos * hs
                    part_w = wof[rem(grp + NY - y, NY), cc * hs : (cc + 1) * hs, :]
                    o += jnp.dot(mixs[rows, at : at + hs], part_w, preferred_element_type=F32)
            outs[rows, :] = o.astype(BF16)

            @pl.when(at_home)
            def _(rows=rows):
                fetch(outs.at[rows, :], out.at[rows, :], 3)

            @pl.when(jnp.logical_not(at_home))
            def _(u=u):
                o_copy(u).start()

    @pl.when(at_home)
    def _():
        done(outs, lsem.at[3])

    @pl.when(jnp.logical_not(at_home))
    def _():
        done(outs, osend.at[0])

    @pl.when(jnp.logical_not(at_home))
    def _():
        done(outs, orecv.at[0])

    done(outs, psend.at[0])
    done(outs, dsend.at[0])
    done(outs, fsend.at[0])

    @pl.when(is_source)
    def _():
        done(xbuf.at[:, pl.ds(0, 2 * fs)], tsend.at[0])

    @pl.when(is_main)
    def _():
        done(xbuf, tsend.at[1])

    @pl.when(not_source)
    def _():
        done(xbuf.at[:, pl.ds(0, fs)], tsend.at[0])
        done(wbuf.at[pl.ds(0, fs), pl.ds(0, 2 * gw)], wcs.at[0])

    done(wbuf.at[pl.ds(0, wr), pl.ds(0, nh)], wys.at[0])
    done(wbuf.at[pl.ds(0, (NZ - 1) * wr), pl.ds(0, nh)], wzs.at[0])
    done(wbuf.at[pl.ds(0, 2 * NZ * wr), pl.ds(0, 2 * hs)], wxs.at[0])
    done(wbuf.at[pl.ds(0, 2 * NZ * wr), pl.ds(0, hs)], wxs.at[1])
    done(wbuf.at[pl.ds(0, fs), pl.ds(0, hs)], wxs.at[2])
    g_copy().wait_send()

    done(wof.at[2, pl.ds(0, br), :], o0s.at[0])
    done(wof.at[2, pl.ds(0, (NZ - 1) * br), :], o1s.at[0])
    done(wof.at[2, pl.ds(0, (NX - 1) * NZ * br), :], o2s.at[0])
    done(wof.at[pl.ds(0, 2)], o3s.at[0])
    done(ga.at[pl.ds(0, NE - 1)], asend.at[0])
    done(gc.at[pl.ds(0, NE - 1)], csend.at[0])
    for n in range(1, NZ):

        @pl.when(z == NZ - 1 - n)
        def _(n=n):
            done(gb.at[pl.ds(0, n)], bsend.at[0])


def on_device(tokens, w_query, w_key, w_value, w_out, mix_logit):
    seg, fs = tokens.shape
    heads = mix_logit.shape[0]
    gw = w_query.shape[1]
    hs = gw // heads
    pr = heads * hs // NE
    hbm = pl.BlockSpec(memory_space=pl.ANY)
    dma = pltpu.SemaphoreType.DMA
    return pl.pallas_call(
        kernel,
        out_shape=jax.ShapeDtypeStruct((seg, fs), BF16),
        in_specs=[hbm] * 5 + [pl.BlockSpec(memory_space=pltpu.SMEM)],
        out_specs=hbm,
        scratch_shapes=[
            pltpu.VMEM((seg, NY * fs), BF16),
            pltpu.VMEM((NY * fs, 3 * gw), BF16),
            pltpu.VMEM((seg, 3 * gw), F32),
            pltpu.VMEM((heads, seg, hs), BF16),
            pltpu.VMEM((heads, seg, hs), BF16),
            pltpu.VMEM((heads, seg, hs), BF16),
            pltpu.VMEM((heads, seg, hs), F32),
            pltpu.VMEM((NY, gw, fs), BF16),
            pltpu.VMEM((heads, hs, hs), F32),
            pltpu.VMEM((heads, 8, hs), F32),
            pltpu.VMEM((NE, 2 * pr + 16, hs // 2), BF16),
            pltpu.VMEM((NE, 2 * pr + 16, hs // 2), BF16),
            pltpu.VMEM((2 * pr + 16, hs // 2), BF16),
            pltpu.VMEM((NZ, 2 * pr + 16, hs // 2), BF16),
            pltpu.VMEM((NE, 2 * pr + 16, hs // 2), BF16),
            pltpu.VMEM((NE, 2 * pr + 16, hs // 2), BF16),
            pltpu.VMEM((heads, hs, hs), BF16),
            pltpu.VMEM((heads, hs, hs), BF16),
            pltpu.VMEM((seg, NY * gw), BF16),
            pltpu.VMEM((seg, fs), BF16),
            pltpu.VMEM((8, hs), F32),
            pltpu.VMEM((8, hs), F32),
            dma((4,)),
            dma((2,)), dma((3, 4)),
            dma((1,)), dma((2,)),
            dma((1,)), dma((NZ,)), dma((1,)),
            dma((3,)), dma((3,)),
            dma((1,)), dma((2,)),
            dma((1,)), dma((1,)),
            dma((1,)), dma((1,)),
            dma((1,)), dma((1,)),
            dma((1,)), dma((2,)),
            dma((1,)), dma((1,)),
            dma((1,)), dma((1,)),
            dma((1,)), dma((1,)),
            dma((1,)), dma((1,)),
            dma((1,)), dma((NU,)),
            dma((1,)), dma((NU,)),
            dma((1,)),
            dma((1,)), dma((1,)),
        ],
        compiler_params=pltpu.CompilerParams(
            collective_id=0, has_side_effects=True, vmem_limit_bytes=52 * 2**20
        ),
    )(tokens, w_query, w_key, w_value, w_out, mix_logit)


def solution(mesh):
    torus = Mesh(mesh.devices.reshape(NZ, NX, NC, NY), ("z", "x", "c", "y"))
    return jax.shard_map(
        on_device,
        mesh=torus,
        in_specs=(P(SEQ, "y"), P(None, "y"), P(None, "y"), P(None, "y"), P("y", None), P("y")),
        out_specs=P(SEQ, "y"),
        check_vma=False,
    )
```

time: 94.3 us -> 88.7 us (0.941)
  Pallas kernels: 92.6 us -> 87 us
    pallas_call x1, Pallas kernels: 92.6 us -> 87 us  [on_device(): pl.pallas_call(kernel, out_shape=jax.ShapeDtypeStruct((seg, fs), BF16), i...]
where the time goes in v5:
time: 88.7 us; the launch traced here: 88.6 us
  Pallas kernels  87 us (98%)
  local copies, waits for them, and re-layouts  1.63 us (2%)
    pallas_call x1, Pallas kernels, on_device(): pl.pallas_call(kernel, out_shape=jax.ShapeDtypeStruct((seg, fs), BF16), i...  87 us

profile of v5, /device:TPU:1, one launch (start us, length us, event | category | flops | bytes accessed | tf_op | source)
XLA Modules:
  0.0 88.6 jit_solution(9926431200746229680)
XLA Ops:
  0.0 0.0 copy-start
  0.0 0.7 copy-done
  0.7 87.0 %shard_map.64 = bf16[1024,512]{1,0:T(8,128)(2,1)S(1)} custom-call(bf16[1024,512]{1,0:T(8,128)(2,1)} %tok.1, bf16[2048,512]{1,0:T(8,128)(2,1)} %wq.1, bf16[2048,512]{1,0:T(8,128)(2,1)} %wk.1, bf16[2048,512]{1,0:T(8,128)(2,1)} %wv.1, bf16[512,2048]{1,0:T(8,128)(2,1)} %wo.1, f32[2]{0:T(128)S(1)} %copy-done), custom_call_target="tpu_custom_call" | custom-call | tf_op jit(solution)/shard_map/pallas_call | solution.py:565
  87.6 1.0 %copy.8 = bf16[1024,512]{1,0:T(8,128)(2,1)} copy(bf16[1024,512]{1,0:T(8,128)(2,1)S(1)} %shard_map.64) | data formatting | bytes 2097152
Async XLA Ops:
  0.0 0.7 copy-start

commit v6 on v5

--- a/solution.py
+++ b/solution.py
@@ -119,7 +119,7 @@
 
     def t_cross(k):
         return remote(
-            tok.at[chunk(k), :], xbuf.at[chunk(k), block(y)], tsend.at[0], trecv.at[0, k], {"y": cross, "c": 1}
+            tok.at[chunk(k), :], xbuf.at[chunk(k), block(y)], tsend.at[0], trecv.at[3, k], {"y": cross, "c": 1}
         )
 
     def t_on(k):
@@ -219,7 +219,6 @@
         for i in (0, 2):
             for ct in (1, 0):
                 w_cross(i, ct).start()
-        o_cross().start()
 
     macc[...] = jnp.zeros_like(macc)
     nacc[...] = jnp.zeros_like(nacc)
@@ -249,21 +248,18 @@
 
     forward_at = {0: (1, 7), 1: (2, 6), 2: (3, 5), 3: (4,)}
     for k in range(4):
-        done(xbuf.at[chunk(k), pl.ds(0, 2 * fs)], trecv.at[0, k])
+        t_wait(k, 3, cross)
 
         @pl.when(is_main)
         def _(k=k):
             t_on(k).start()
-            t_sib(k, 0, cross).start()
-            t_sib(k, 0, part).start()
+            t_sib(k, 3, cross).start()
 
         for d in forward_at[k]:
             w_z(0, d).wait_recv()
             w_xs(d)
         rows = chunk(k)
-        add = jnp.dot(xbuf[rows, block(part)], wbuf[block(part), 0:nh], preferred_element_type=F32)
-        add += jnp.dot(xbuf[rows, block(cross)], wbuf[block(cross), 0:nh], preferred_element_type=F32)
-        acc[rows, 0:nh] += add
+        acc[rows, 0:nh] += jnp.dot(xbuf[rows, block(cross)], wbuf[block(cross), 0:nh], preferred_element_type=F32)
 
     def finish(h, rows, kv):
         kv = kv.astype(BF16)
@@ -300,6 +296,12 @@
 
     last = NY - 1 - part
     for k in range(4):
+        t_wait(k, 0, part)
+
+        @pl.when(is_main)
+        def _(k=k):
+            t_sib(k, 0, part).start()
+
         if k == 3:
             done(wbuf.at[pl.ds(0, 2 * NZ * wr), pl.ds(0, 2 * hs)], wxr.at[0])
             done(wbuf.at[pl.ds(0, fs), pl.ds(0, hs)], wxr.at[2])
@@ -317,8 +319,10 @@
 
         rows = chunk(k)
         acc[rows, ck] = jnp.dot(xbuf[rows, block(x)], wbuf[block(x), ck], preferred_element_type=F32)
-        add = jnp.dot(xbuf[rows, block(last)], wbuf[block(last), ok], preferred_element_type=F32)
-        finish(0, rows, acc[rows, ok] + add)
+        add = jnp.dot(xbuf[rows, block(part)], wbuf[block(part), 0:nh], preferred_element_type=F32)
+        kv = jnp.dot(xbuf[rows, block(last)], wbuf[block(last), ok], preferred_element_type=F32)
+        acc[rows, oq] += add[:, oq]
+        finish(0, rows, acc[rows, ok] + (kv + add[:, ok]))
 
     cross_rows(3)
 
@@ -349,6 +353,11 @@
         a_copy(i).start()
     ga[e] = mt[e]
     o_pair().start()
+
+    @pl.when(not_source)
+    def _():
+        o_cross().start()
+
     pl.when(c == 0)(q_forward)
 
     scale = 1.0 / hs**0.5
@@ -591,7 +600,7 @@
             pltpu.VMEM((8, hs), F32),
             pltpu.VMEM((8, hs), F32),
             dma((4,)),
-            dma((2,)), dma((3, 4)),
+            dma((2,)), dma((4, 4)),
             dma((1,)), dma((2,)),
             dma((1,)), dma((NZ,)), dma((1,)),
             dma((3,)), dma((3,)),

time: 88.7 us -> 85 us (0.958)
  Pallas kernels: 87 us -> 83.2 us
    pallas_call x1, Pallas kernels: 87 us -> 83.2 us  [on_device(): pl.pallas_call(kernel, out_shape=jax.ShapeDtypeStruct((seg, fs), BF16), i...]
where the time goes in v6:
time: 85 us; the launch traced here: 84.9 us
  Pallas kernels  83.2 us (98%)
  local copies, waits for them, and re-layouts  1.63 us (2%)
    pallas_call x1, Pallas kernels, on_device(): pl.pallas_call(kernel, out_shape=jax.ShapeDtypeStruct((seg, fs), BF16), i...  83.2 us

profile of v6, /device:TPU:1, one launch (start us, length us, event | category | flops | bytes accessed | tf_op | source)
XLA Modules:
  0.0 84.9 jit_solution(12714205265832612421)
XLA Ops:
  0.0 0.0 copy-start
  0.0 0.7 copy-done
  0.7 83.2 %shard_map.64 = bf16[1024,512]{1,0:T(8,128)(2,1)S(1)} custom-call(bf16[1024,512]{1,0:T(8,128)(2,1)} %tok.1, bf16[2048,512]{1,0:T(8,128)(2,1)} %wq.1, bf16[2048,512]{1,0:T(8,128)(2,1)} %wk.1, bf16[2048,512]{1,0:T(8,128)(2,1)} %wv.1, bf16[512,2048]{1,0:T(8,128)(2,1)} %wo.1, f32[2]{0:T(128)S(1)} %copy-done), custom_call_target="tpu_custom_call" | custom-call | tf_op jit(solution)/shard_map/pallas_call | solution.py:574
  83.9 1.0 %copy.8 = bf16[1024,512]{1,0:T(8,128)(2,1)} copy(bf16[1024,512]{1,0:T(8,128)(2,1)S(1)} %shard_map.64) | data formatting | bytes 2097152
Async XLA Ops:
  0.0 0.7 copy-start

commit v7 on v6

--- a/solution.py
+++ b/solution.py
@@ -79,6 +79,12 @@
     def chunk(j):
         return pl.ds(pl.multiple_of(j * rc, rc), rc)
 
+    pieces = [(0, rc), (rc, rc), (2 * rc, rc), (3 * rc, rc // 2), (3 * rc + rc // 2, rc // 2)]
+    nk = len(pieces)
+
+    def part_rows(k):
+        return pl.ds(*pieces[k])
+
     def block(f):
         return pl.ds(pl.multiple_of(f * fs, fs), fs)
 
@@ -114,20 +120,20 @@
 
     def t_pair(k):
         return remote(
-            tok.at[chunk(k), :], xbuf.at[chunk(k), block(y)], tsend.at[0], trecv.at[0, k], {"y": part, "c": 1}
+            tok.at[part_rows(k), :], xbuf.at[part_rows(k), block(y)], tsend.at[0], trecv.at[0, k], {"y": part, "c": 1}
         )
 
     def t_cross(k):
         return remote(
-            tok.at[chunk(k), :], xbuf.at[chunk(k), block(y)], tsend.at[0], trecv.at[3, k], {"y": cross, "c": 1}
+            tok.at[part_rows(k), :], xbuf.at[part_rows(k), block(y)], tsend.at[0], trecv.at[3, k], {"y": cross, "c": 1}
         )
 
     def t_on(k):
-        ref = xbuf.at[chunk(k), block(cross)]
+        ref = xbuf.at[part_rows(k), block(cross)]
         return remote(ref, ref, tsend.at[1], trecv.at[1, k], {"y": part})
 
     def t_sib(k, kind, f):
-        ref = xbuf.at[chunk(k), block(f)]
+        ref = xbuf.at[part_rows(k), block(f)]
         return remote(ref, ref, tsend.at[1], trecv.at[kind, k], sibling)
 
     def t_own():
@@ -159,7 +165,10 @@
     def w_xs(d):
         w_x(0, 1, d).start()
         w_x(0, 3, d).start()
-        w_x(2, 2, d).start()
+
+        @pl.when(c == 0)
+        def _():
+            w_x(2, 2, d).start()
 
     def w_cross(i, ct):
         return remote(
@@ -202,13 +211,13 @@
 
     @pl.when(is_source)
     def _():
-        for k in range(4):
+        for k in range(nk):
             t_pair(k).start()
         t_own().start()
 
     @pl.when(not_source)
     def _():
-        for k in range(4):
+        for k in range(nk):
             t_cross(k).start()
 
     w_piece(2).start()
@@ -216,9 +225,8 @@
 
     @pl.when(not_source)
     def _():
-        for i in (0, 2):
-            for ct in (1, 0):
-                w_cross(i, ct).start()
+        for i, ct in ((0, 1), (1, 1), (0, 0), (2, 1), (2, 0)):
+            w_cross(i, ct).start()
 
     macc[...] = jnp.zeros_like(macc)
     nacc[...] = jnp.zeros_like(nacc)
@@ -246,8 +254,8 @@
     w_xs(0)
     lax.fori_loop(2, 4, own_dot, 0)
 
-    forward_at = {0: (1, 7), 1: (2, 6), 2: (3, 5), 3: (4,)}
-    for k in range(4):
+    forward_at = {0: (1, 7), 1: (2, 6), 2: (3, 5), 3: (4,), 4: ()}
+    for k in range(nk):
         t_wait(k, 3, cross)
 
         @pl.when(is_main)
@@ -258,7 +266,7 @@
         for d in forward_at[k]:
             w_z(0, d).wait_recv()
             w_xs(d)
-        rows = chunk(k)
+        rows = part_rows(k)
         acc[rows, 0:nh] += jnp.dot(xbuf[rows, block(cross)], wbuf[block(cross), 0:nh], preferred_element_type=F32)
 
     def finish(h, rows, kv):
@@ -268,10 +276,10 @@
         v_s[h, rows, :] = val
         fk = feature(key.astype(F32)).astype(BF16)
         macc[h] += lax.dot_general(fk, val, TN, preferred_element_type=F32)
-        nacc[h] += jnp.sum(fk.astype(F32).reshape(rc // 8, 8, hs), axis=0)
-
-    def cross_rows(j):
-        rows = chunk(j)
+        nacc[h] += jnp.sum(fk.astype(F32).reshape(-1, 8, hs), axis=0)
+
+    def cross_rows(k):
+        rows = part_rows(k)
         kv = acc[rows, ck]
         for i in range(1, NX):
             f = block(rem(x + i, NX))
@@ -295,36 +303,49 @@
             w_x(1, 3, d).start()
 
     last = NY - 1 - part
-    for k in range(4):
+    for k in range(nk):
+        if k == 2:
+
+            @pl.when(c == 1)
+            def _():
+                done(wbuf.at[pl.ds(0, 2 * NZ * wr), pl.ds(0, 2 * hs)], wxr.at[0])
+                done(wbuf.at[pl.ds(0, fs), pl.ds(0, 2 * hs)], wcr.at[0])
+                cross_rows(0)
+                cross_rows(1)
+
+        if k == 3:
+
+            @pl.when(c == 0)
+            def _():
+                done(wbuf.at[pl.ds(0, 2 * NZ * wr), pl.ds(0, 2 * hs)], wxr.at[0])
+                done(wbuf.at[pl.ds(0, fs), pl.ds(0, hs)], wxr.at[2])
+                done(wbuf.at[pl.ds(0, fs), pl.ds(0, hs)], wcr.at[0])
+                cross_rows(0)
+                cross_rows(1)
+
+            cross_rows(2)
+            pl.when(c == 1)(q_forward)
+
         t_wait(k, 0, part)
 
         @pl.when(is_main)
         def _(k=k):
             t_sib(k, 0, part).start()
 
-        if k == 3:
-            done(wbuf.at[pl.ds(0, 2 * NZ * wr), pl.ds(0, 2 * hs)], wxr.at[0])
-            done(wbuf.at[pl.ds(0, fs), pl.ds(0, hs)], wxr.at[2])
-            done(wbuf.at[pl.ds(0, fs), pl.ds(0, hs)], wcr.at[0])
-
-            for j in range(3):
-                cross_rows(j)
-            pl.when(c == 1)(q_forward)
-
         t_wait(k, 1, last)
 
         @pl.when(is_main)
         def _(k=k):
             t_sib(k, 1, last).start()
 
-        rows = chunk(k)
+        rows = part_rows(k)
         acc[rows, ck] = jnp.dot(xbuf[rows, block(x)], wbuf[block(x), ck], preferred_element_type=F32)
         add = jnp.dot(xbuf[rows, block(part)], wbuf[block(part), 0:nh], preferred_element_type=F32)
         kv = jnp.dot(xbuf[rows, block(last)], wbuf[block(last), ok], preferred_element_type=F32)
         acc[rows, oq] += add[:, oq]
         finish(0, rows, acc[rows, ok] + (kv + add[:, ok]))
-
-    cross_rows(3)
+        if k >= 3:
+            cross_rows(k)
 
     per_head, hw = hs // pr, hs // 2
     norms = []
@@ -412,7 +433,6 @@
             o_x(i).start()
 
     done(wof.at[2, pl.ds(0, (NZ - 1) * br), :], o1r.at[0])
-    pl.when(c == 0)(bulk)
 
     done(wbuf.at[pl.ds(0, fs), pl.ds(0, hs)], wcr.at[1])
     done(wbuf.at[pl.ds(0, 2 * NZ * wr), pl.ds(0, hs)], wxr.at[1])
@@ -441,9 +461,10 @@
     for i in range(1, NE):
         c_copy(i).start()
     gc[e] = pc[e]
+    pl.when(c == 0)(bulk)
+
+    done(gc.at[pl.ds(0, NE - 1)], crecv.at[0])
     pl.when(c == 1)(bulk)
-
-    done(gc.at[pl.ds(0, NE - 1)], crecv.at[0])
     for h in range(heads):
         slot = m if h == 0 else 1 - m
         for p in range(per_head):
@@ -541,13 +562,17 @@
     @pl.when(not_source)
     def _():
         done(xbuf.at[:, pl.ds(0, fs)], tsend.at[0])
-        done(wbuf.at[pl.ds(0, fs), pl.ds(0, 2 * gw)], wcs.at[0])
+        done(wbuf.at[pl.ds(0, fs), pl.ds(0, 5 * hs)], wcs.at[0])
 
     done(wbuf.at[pl.ds(0, wr), pl.ds(0, nh)], wys.at[0])
     done(wbuf.at[pl.ds(0, (NZ - 1) * wr), pl.ds(0, nh)], wzs.at[0])
     done(wbuf.at[pl.ds(0, 2 * NZ * wr), pl.ds(0, 2 * hs)], wxs.at[0])
     done(wbuf.at[pl.ds(0, 2 * NZ * wr), pl.ds(0, hs)], wxs.at[1])
-    done(wbuf.at[pl.ds(0, fs), pl.ds(0, hs)], wxs.at[2])
+
+    @pl.when(c == 0)
+    def _():
+        done(wbuf.at[pl.ds(0, fs), pl.ds(0, hs)], wxs.at[2])
+
     g_copy().wait_send()
 
     done(wof.at[2, pl.ds(0, br), :], o0s.at[0])
@@ -600,7 +625,7 @@
             pltpu.VMEM((8, hs), F32),
             pltpu.VMEM((8, hs), F32),
             dma((4,)),
-            dma((2,)), dma((4, 4)),
+            dma((2,)), dma((4, 5)),
             dma((1,)), dma((2,)),
             dma((1,)), dma((NZ,)), dma((1,)),
             dma((3,)), dma((3,)),

time: 85 us -> 83.5 us (0.982)
  Pallas kernels: 83.2 us -> 81.1 us
    pallas_call x1, Pallas kernels: 83.2 us -> 81.1 us  [on_device(): pl.pallas_call(kernel, out_shape=jax.ShapeDtypeStruct((seg, fs), BF16), i...]
where the time goes in v7:
time: 83.5 us; the launch traced here: 82.8 us
  Pallas kernels  81.1 us (97%)
  local copies, waits for them, and re-layouts  1.63 us (2%)
    pallas_call x1, Pallas kernels, on_device(): pl.pallas_call(kernel, out_shape=jax.ShapeDtypeStruct((seg, fs), BF16), i...  81.1 us

profile of v7, /device:TPU:1, one launch (start us, length us, event | category | flops | bytes accessed | tf_op | source)
XLA Modules:
  0.0 82.8 jit_solution(4773804437877883367)
XLA Ops:
  0.0 0.0 copy-start
  0.0 0.7 copy-done
  0.7 81.1 %shard_map.64 = bf16[1024,512]{1,0:T(8,128)(2,1)S(1)} custom-call(bf16[1024,512]{1,0:T(8,128)(2,1)} %tok.1, bf16[2048,512]{1,0:T(8,128)(2,1)} %wq.1, bf16[2048,512]{1,0:T(8,128)(2,1)} %wk.1, bf16[2048,512]{1,0:T(8,128)(2,1)} %wv.1, bf16[512,2048]{1,0:T(8,128)(2,1)} %wo.1, f32[2]{0:T(128)S(1)} %copy-done), custom_call_target="tpu_custom_call" | custom-call | tf_op jit(solution)/shard_map/pallas_call | solution.py:599
  81.8 1.0 %copy.8 = bf16[1024,512]{1,0:T(8,128)(2,1)} copy(bf16[1024,512]{1,0:T(8,128)(2,1)S(1)} %shard_map.64) | data formatting | bytes 2097152
Async XLA Ops:
  0.0 0.7 copy-start

commit v8 on v7

--- a/solution.py
+++ b/solution.py
@@ -461,10 +461,9 @@
     for i in range(1, NE):
         c_copy(i).start()
     gc[e] = pc[e]
-    pl.when(c == 0)(bulk)
 
     done(gc.at[pl.ds(0, NE - 1)], crecv.at[0])
-    pl.when(c == 1)(bulk)
+    bulk()
     for h in range(heads):
         slot = m if h == 0 else 1 - m
         for p in range(per_head):

time: 83.5 us -> 84.9 us (1.017)
  Pallas kernels: 81.1 us -> 83.2 us
    pallas_call x1, Pallas kernels: 81.1 us -> 83.2 us  [on_device(): pl.pallas_call(kernel, out_shape=jax.ShapeDtypeStruct((seg, fs), BF16), i...]
where the time goes in v8:
time: 84.9 us
  Pallas kernels  83.2 us (98%)
  local copies, waits for them, and re-layouts  1.63 us (2%)
    pallas_call x1, Pallas kernels, on_device(): pl.pallas_call(kernel, out_shape=jax.ShapeDtypeStruct((seg, fs), BF16), i...  83.2 us

profile of v8, /device:TPU:1, one launch (start us, length us, event | category | flops | bytes accessed | tf_op | source)
XLA Modules:
  0.0 84.9 jit_solution(15173976290928834994)
XLA Ops:
  0.0 0.0 copy-start
  0.0 0.7 copy-done
  0.7 83.2 %shard_map.64 = bf16[1024,512]{1,0:T(8,128)(2,1)S(1)} custom-call(bf16[1024,512]{1,0:T(8,128)(2,1)} %tok.1, bf16[2048,512]{1,0:T(8,128)(2,1)} %wq.1, bf16[2048,512]{1,0:T(8,128)(2,1)} %wk.1, bf16[2048,512]{1,0:T(8,128)(2,1)} %wv.1, bf16[512,2048]{1,0:T(8,128)(2,1)} %wo.1, f32[2]{0:T(128)S(1)} %copy-done), custom_call_target="tpu_custom_call" | custom-call | tf_op jit(solution)/shard_map/pallas_call | solution.py:598
  83.9 1.0 %copy.8 = bf16[1024,512]{1,0:T(8,128)(2,1)} copy(bf16[1024,512]{1,0:T(8,128)(2,1)S(1)} %shard_map.64) | data formatting | bytes 2097152
Async XLA Ops:
  0.0 0.7 copy-start
